TPU v7x, 32 devices: a whole 2x2x4 slice. The times are simulated.
32 devices in a mesh: dp: 2 (over x), tp: 4 (over z), cp: 4 (over y, core).
Axes of the slice: x: 2, y: 2, z: 4, core: 2. Of those that a mesh axis runs over, the one named last changes fastest.
Arguments:
- x: bfloat16 [16384, 4096], P(('dp', 'cp', 'tp')), parts along dimension 0
- w_q: bfloat16 [4096, 4096], P(None, 'tp')
- w_k: bfloat16 [4096, 1024], P(None, 'tp')
- w_v: bfloat16 [4096, 1024], P(None, 'tp')
- w_o: bfloat16 [4096, 4096], P('tp')
Outputs:
- output: bfloat16 [16384, 4096], P(('dp', 'cp', 'tp')), parts along dimension 0
There are 2 independent parts. A program takes and returns all parts, laid end to end along the dimension named above; an argument that names none is the same for every part.
All inputs are finite; a program needn't handle non-finite values.
Results may differ from a plain program's by a relative error of at most 0.0055191.
Values are sent between devices in bfloat16 or wider.
A program may use at most 1 GiB of HBM per device.

v0:
```python
import jax
import jax.numpy as jnp
from jax import lax
from jax.sharding import PartitionSpec as P

HEAD_DIM = 128


def block_scores(q_part, k_part):
    raw_scores = jnp.einsum("qhge,khe->hgqk", q_part, k_part, preferred_element_type=jnp.float32)
    return raw_scores * (HEAD_DIM ** -0.5)


def merge_block(soft_state, scores, v_part):
    run_max, run_sum, run_acc = soft_state
    new_max = jnp.maximum(run_max, scores.max(axis=-1))
    rescale = jnp.exp(run_max - new_max)
    p_block = jnp.exp(scores - new_max[..., None])
    new_sum = run_sum * rescale + p_block.sum(axis=-1)
    new_acc = run_acc * rescale[..., None] + jnp.einsum("hgqk,khe->hgqe", p_block.astype(jnp.bfloat16), v_part, preferred_element_type=jnp.float32)
    return new_max, new_sum, new_acc


def solution(mesh):
    cp_size = mesh.shape["cp"]
    row_spec = P(("dp", "cp", "tp"), None)

    def local_layer(x_loc, w_q, w_k, w_v, w_o):
        model_width = x_loc.shape[1]
        kv_local = w_k.shape[1] // HEAD_DIM
        group_size = w_q.shape[1] // w_k.shape[1]
        x_block = lax.all_gather(x_loc, "tp", axis=0, tiled=True)
        piece_len = x_block.shape[0] // 2
        q_all = jnp.dot(x_block, w_q, preferred_element_type=jnp.float32).astype(jnp.bfloat16).reshape(2, piece_len, kv_local, group_size, HEAD_DIM)
        k_all = jnp.dot(x_block, w_k, preferred_element_type=jnp.float32).astype(jnp.bfloat16).reshape(2, piece_len, kv_local, HEAD_DIM)
        v_all = jnp.dot(x_block, w_v, preferred_element_type=jnp.float32).astype(jnp.bfloat16).reshape(2, piece_len, kv_local, HEAD_DIM)
        q_low = q_all[0]
        q_high = q_all[1]
        cp_rank = lax.axis_index("cp")
        offsets = jnp.arange(piece_len)
        pos_low = cp_rank * piece_len + offsets
        pos_high = (2 * cp_size - 1 - cp_rank) * piece_len + offsets
        pos_both = jnp.concatenate([pos_low, pos_high])
        stat_shape = (kv_local, group_size, piece_len)
        empty_state = (jnp.full(stat_shape, -jnp.inf, jnp.float32), jnp.zeros(stat_shape, jnp.float32), jnp.zeros(stat_shape + (HEAD_DIM,), jnp.float32))
        k_flat = k_all.reshape(2 * piece_len, kv_local, HEAD_DIM)
        v_flat = v_all.reshape(2 * piece_len, kv_local, HEAD_DIM)
        low_scores = jnp.where(pos_low[:, None] >= pos_low[None, :], block_scores(q_low, k_all[0]), -jnp.inf)
        high_scores = jnp.where(pos_high[:, None] >= pos_both[None, :], block_scores(q_high, k_flat), -jnp.inf)
        own_states = (merge_block(empty_state, low_scores, v_all[0]), merge_block(empty_state, high_scores, v_flat))

        def earlier_source(states, kv_src):
            state_low, state_high = states
            k_src = kv_src[0, 0]
            v_src = kv_src[1, 0]
            return (merge_block(state_low, block_scores(q_low, k_src), v_src), merge_block(state_high, block_scores(q_high, k_src), v_src))

        def later_source(states, kv_src):
            state_low, state_high = states
            k_src = kv_src[0].reshape(2 * piece_len, kv_local, HEAD_DIM)
            v_src = kv_src[1].reshape(2 * piece_len, kv_local, HEAD_DIM)
            return (state_low, merge_block(state_high, block_scores(q_high, k_src), v_src))

        shift_pairs = [(dev_idx, (dev_idx + 1) % cp_size) for dev_idx in range(cp_size)]

        def kv_step(step_idx, loop_carry):
            states, kv_held = loop_carry
            kv_held = lax.ppermute(kv_held, "cp", shift_pairs)
            source = (cp_rank - step_idx) % cp_size
            states = lax.cond(source < cp_rank, earlier_source, later_source, states, kv_held)
            return states, kv_held

        kv_pair = jnp.stack([k_all, v_all])
        final_carry = lax.fori_loop(1, cp_size, kv_step, (own_states, kv_pair))
        state_low, state_high = final_carry[0]
        out_low = (state_low[2] / state_low[1][..., None]).astype(jnp.bfloat16)
        out_high = (state_high[2] / state_high[1][..., None]).astype(jnp.bfloat16)
        attn_out = jnp.stack([out_low, out_high], axis=2)
        w_o_heads = w_o.reshape(kv_local, group_size, HEAD_DIM, model_width)
        partial = jnp.einsum("hgsqe,hged->sqd", attn_out, w_o_heads, preferred_element_type=jnp.float32).reshape(2 * piece_len, model_width)
        y_loc = lax.psum_scatter(partial, "tp", scatter_dimension=0, tiled=True)
        return y_loc.astype(jnp.bfloat16)

    return jax.shard_map(local_layer, mesh=mesh, in_specs=(row_spec, P(None, "tp"), P(None, "tp"), P(None, "tp"), P("tp", None)), out_specs=row_spec, check_vma=False)
```

profile of v0, /device:TPU:0, one launch (start us, length us, event | category | flops | bytes accessed | tf_op | source)
XLA Modules:
  0.0 1437.2 jit_solution(7310391283044161090)
XLA Ops:
  8.0 2.4 broadcast_compare_fusion
  10.4 289.1 %all-gather.2.cloned.1.call-done = bf16[2048,4096]{1,0:T(8,128)(2,1)} async-done(((bf16[512,4096]{1,0:T(8,128)(2,1)}), bf16[2048,4096]{1,0:T(8,128)(2,1)}) %all-gather.2.cloned.1.call-update) | async-done | bytes 16777232 | tf_op jit(solution)/shard_map/all_gather | solution.py:32
  299.5 9.3 convolution_convert_fusion.1
  308.8 1.9 slice.36
  310.6 2.6 stack_reshape.7
  313.3 10.9 convolution_convert_fusion.2
  325.1 1.6 stack_reshape.6
  326.7 23.0 %convolution_convert_fusion = bf16[2048,1024]{0,1:T(8,128)(2,1)S(1)} fusion(bf16[2048,4096]{1,0:T(8,128)(2,1)} %all-gather.2.cloned.1.call-done, bf16[4096,1024]{1,0:T(8,128)(2,1)} %param.10), kind=kOutput, calls=%fused_computation.64 | convolution fusion | flops 17181966336 | bytes 29360128 | tf_op jit(solution)/shard_map/dot_general | solution.py:34
  349.7 1.8 fusion.65
  351.5 2.6 copy.21
  354.1 15.2 %fusion.46 = (f32[2,4,1024]{2,1,0:T(4,128)}, f32[2,1024,1024,4]{2,1,3,0:T(8,128)}) fusion(pred[1024,1024]{0,1:T(8,128)(4,1)S(1)} %broadcast_compare_fusion.1, bf16[1024,2,128,1]{0,2,3,1:T(8,128)(2,1)} %bitcast.186, bf16[1024,2,4,128]{0,3,2,1:T(8,128)(2,1)S(1)} %bitcast.167), kind=kOutput, calls=%fused_computation.55 | convolution fusion | flops 2172641280 | bytes 37257216 | tf_op jit(solution)/shard_map/qhge,khe->hgqk/dot_general | solution.py:10
  369.3 14.4 fusion.45
  384.4 4.0 copy.20
  388.4 25.7 %fusion.40 = (f32[2,4,1024]{2,1,0:T(4,128)S(1)}, f32[2,2048,1024,4]{2,1,3,0:T(8,128)}) fusion(pred[1024,2048]{0,1:T(8,128)(4,1)S(1)} %copy-done.4, bf16[2048,2,128,1]{0,2,3,1:T(8,128)(2,1)} %bitcast.185, bf16[1024,2,4,128]{0,3,2,1:T(8,128)(2,1)} %bitcast.173), kind=kOutput, calls=%fused_computation.48 | convolution fusion | flops 4345290752 | bytes 72384512 | tf_op jit(solution)/shard_map/qhge,khe->hgqk/dot_general | solution.py:10
  414.1 21.6 %fusion.39 = f32[2,4,1024]{2,1,0:T(4,128)S(1)} fusion(f32[2,2048,1024,4]{2,1,3,0:T(8,128)} %get-tuple-element.430, f32[2,4,1024]{2,1,0:T(4,128)S(1)} %get-tuple-element.534, pred[1024,2048]{0,1:T(8,128)(4,1)S(1)} %copy-done.4), kind=kLoop, calls=%fused_computation.47 | loop fusion | flops 67100672 | bytes 69271552 | tf_op jit(solution)/shard_map/reduce_sum | solution.py:19
  435.7 3.7 copy.19
  439.3 3.6 copy.18
  443.0 17.2 %broadcast_add_fusion = f32[2,4,1024,128]{3,2,1,0:T(8,128)} fusion(f32[2,4,1024]{2,1,0:T(4,128)S(1)} %get-tuple-element.425, bf16[1024,2,128,1]{0,2,3,1:T(8,128)(2,1)} %bitcast.189, f32[2,1024,1024,4]{2,1,3,0:T(8,128)} %get-tuple-element.428, f32[2,4,1024]{2,1,0:T(4,128)} %get-tuple-element.531, pred[1024,1024]{0,1:T(8,128)(4,1)S(1)} %broadcast_compare_fusion.1), kind=kOutput, calls=%fused_computation.69 | convolution fusion | flops 2182086656 | bytes 39387136 | tf_op jit(solution)/shard_map/hgqk,khe->hgqe/dot_general | solution.py:20
  460.2 28.6 %fusion.51 = f32[2,4,1024,128]{3,2,1,0:T(8,128)} fusion(bf16[2048,2,128,1]{0,2,3,1:T(8,128)(2,1)} %bitcast.184, f32[2,2048,1024,4]{2,1,3,0:T(8,128)} %get-tuple-element.430, f32[2,4,1024]{2,1,0:T(4,128)S(1)} %get-tuple-element.534, pred[1024,2048]{0,1:T(8,128)(4,1)S(1)} %copy-done.4, f32[2,4,1024]{2,1,0:T(4,128)S(1)} %get-tuple-element.423), kind=kOutput, calls=%fused_computation.67 | convolution fusion | flops 4363124736 | bytes 74514432 | tf_op jit(solution)/shard_map/hgqk,khe->hgqe/dot_general | solution.py:20
  488.8 2.8 pad_maximum_fusion
  491.6 341.0 %while.27 = (s32[]{:T(128)}, f32[2,4,1024]{2,1,0:T(4,128)}, f32[2,4,1024]{2,1,0:T(4,128)S(1)}, f32[2,4,1024,128]{3,2,1,0:T(8,128)}, f32[2,4,1024]{2,1,0:T(4,128)...) while((s32[]{:T(128)}, f32[2,4,1024]{2,1,0:T(4,128)}, ...), condition=%wide.region_13.14_spmd, body=%wide.region_4.13_spmd.sunk | while | flops 8728379392 | bytes 246415888 | solution.py:74
  491.9 25.3 %collective-permute-done = bf16[2,2,1024,2,128]{4,2,3,1,0:T(8,128)(2,1)S(1)} collective-permute-done((bf16[2,2,1024,2,128]{4,2,3,1,0:T(8,128)(2,1)}, bf16[2,2,1024,2,128]{4,2,3,1,0:T(8,128)(2,1)S(1)}, u32[]{:S(2)}, u32[]{:S(2)}) %collective-permute-start) | collective-permute-done | bytes 2097184 | tf_op jit(solution)/shard_map/while/body/eval_jaxpr/ppermute | solution.py:68
  517.2 77.1 %conditional.2 = (f32[2,4,1024]{2,1,0:T(4,128)}, f32[2,4,1024]{2,1,0:T(4,128)S(1)}, f32[2,4,1024,128]{3,2,1,0:T(8,128)}, f32[2,4,1024]{2,1,0:T(4,128)}, f32[2,4,...) conditional(s32[]{:T(128)} %convert_element_type.81, (bf16[2,2,1024,2,128]{4,2,3,1,0:T(8,128)(2,1)S(1)}, ...), branch_computations={%region_5.7_spmd, %region_8.12_spmd} | conditional | flops 8728379392 | bytes 233766992 | solution.py:70
  518.4 25.8 %bitcast_reduce_fusion = (f32[2,4,1024]{2,1,0:T(4,128)S(1)}, f32[2,2048,1024,4]{2,1,3,0:T(8,128)}) fusion(bf16[2048,2,128,1]{2,0,3,1:T(8,128)(2,1)} %bitcast.165, bf16[1024,2,4,128]{3,0,2,1:T(8,128)(2,1)} %get-tuple-element.326), kind=kOutput, calls=%fused_computation.1 | convolution fusion | flops 4328513536 | bytes 70287360 | tf_op jit(solution)/shard_map/while/body/eval_jaxpr/cond/branch_0_fun/qhge,khe->hgqk/dot_general | solution.py:10
  544.8 21.4 %fusion.2 = f32[2,4,1024]{2,1,0:T(4,128)S(1)} fusion(f32[2,2048,1024,4]{2,1,3,0:T(8,128)} %get-tuple-element.414, f32[2,4,1024]{2,1,0:T(4,128)} %max.6), kind=kLoop, calls=%fused_computation.4 | loop fusion | flops 50323456 | bytes 67174400 | tf_op jit(solution)/shard_map/while/body/eval_jaxpr/cond/branch_0_fun/reduce_sum | solution.py:19
  567.0 27.3 %multiply_add_fusion = f32[2,4,1024,128]{3,2,1,0:T(8,128)} fusion(f32[2,4,1024,128]{3,2,1,0:T(8,128)} %get-tuple-element.328, bf16[2048,2,128,1]{2,0,3,1:T(8,128)(2,1)S(1)} %bitcast.164, f32[2,2048,1024,4]{2,1,3,0:T(8,128)} %get-tuple-element.414, f32[2,4,1024]{2,1,0:T(4,128)} %max.6, f32[2,4,1024]{2,1,0:T(4,128)S(1)} %bitcast.168), kind=kOutput, calls=%fused_computation.6 | convolution fusion | flops 4347396096 | bytes 76611584 | tf_op jit(solution)/shard_map/while/body/eval_jaxpr/cond/branch_0_fun/hgqk,khe->hgqe/dot_general | solution.py:20
  595.1 1.3 copy.87
  596.4 15.0 %collective-permute-start = (bf16[2,2,1024,2,128]{4,2,3,1,0:T(8,128)(2,1)}, bf16[2,2,1024,2,128]{4,2,3,1,0:T(8,128)(2,1)S(1)}, u32[]{:S(2)}, u32[]{:S(2)}) collective-permute-start(bf16[2,2,1024,2,128]{4,2,3,1,0:T(8,128)(2,1)} %get-tuple-element.552), channel_id=1, source_target_pairs={{0,1},{1,2},{2,3},{3,0},{4,5},{5,6},{6,7},{7,4},{8,9},{9,10},{10,1... | collective-permute-start | bytes 6291464 | tf_op jit(solution)/shard_map/while/body/eval_jaxpr/ppermute | solution.py:68
  611.4 23.9 %collective-permute-done = bf16[2,2,1024,2,128]{4,2,3,1,0:T(8,128)(2,1)S(1)} collective-permute-done((bf16[2,2,1024,2,128]{4,2,3,1,0:T(8,128)(2,1)}, bf16[2,2,1024,2,128]{4,2,3,1,0:T(8,128)(2,1)S(1)}, u32[]{:S(2)}, u32[]{:S(2)}) %collective-permute-start) | collective-permute-done | bytes 2097184 | tf_op jit(solution)/shard_map/while/body/eval_jaxpr/ppermute | solution.py:68
  635.2 77.1 %conditional.2 = (f32[2,4,1024]{2,1,0:T(4,128)}, f32[2,4,1024]{2,1,0:T(4,128)S(1)}, f32[2,4,1024,128]{3,2,1,0:T(8,128)}, f32[2,4,1024]{2,1,0:T(4,128)}, f32[2,4,...) conditional(s32[]{:T(128)} %convert_element_type.81, (bf16[2,2,1024,2,128]{4,2,3,1,0:T(8,128)(2,1)S(1)}, ...), branch_computations={%region_5.7_spmd, %region_8.12_spmd} | conditional | flops 8728379392 | bytes 233766992 | solution.py:70
  636.4 25.8 %bitcast_reduce_fusion = (f32[2,4,1024]{2,1,0:T(4,128)S(1)}, f32[2,2048,1024,4]{2,1,3,0:T(8,128)}) fusion(bf16[2048,2,128,1]{2,0,3,1:T(8,128)(2,1)} %bitcast.165, bf16[1024,2,4,128]{3,0,2,1:T(8,128)(2,1)} %get-tuple-element.326), kind=kOutput, calls=%fused_computation.1 | convolution fusion | flops 4328513536 | bytes 70287360 | tf_op jit(solution)/shard_map/while/body/eval_jaxpr/cond/branch_0_fun/qhge,khe->hgqk/dot_general | solution.py:10
  662.8 21.4 %fusion.2 = f32[2,4,1024]{2,1,0:T(4,128)S(1)} fusion(f32[2,2048,1024,4]{2,1,3,0:T(8,128)} %get-tuple-element.414, f32[2,4,1024]{2,1,0:T(4,128)} %max.6), kind=kLoop, calls=%fused_computation.4 | loop fusion | flops 50323456 | bytes 67174400 | tf_op jit(solution)/shard_map/while/body/eval_jaxpr/cond/branch_0_fun/reduce_sum | solution.py:19
  685.0 27.3 %multiply_add_fusion = f32[2,4,1024,128]{3,2,1,0:T(8,128)} fusion(f32[2,4,1024,128]{3,2,1,0:T(8,128)} %get-tuple-element.328, bf16[2048,2,128,1]{2,0,3,1:T(8,128)(2,1)S(1)} %bitcast.164, f32[2,2048,1024,4]{2,1,3,0:T(8,128)} %get-tuple-element.414, f32[2,4,1024]{2,1,0:T(4,128)} %max.6, f32[2,4,1024]{2,1,0:T(4,128)S(1)} %bitcast.168), kind=kOutput, calls=%fused_computation.6 | convolution fusion | flops 4347396096 | bytes 76611584 | tf_op jit(solution)/shard_map/while/body/eval_jaxpr/cond/branch_0_fun/hgqk,khe->hgqe/dot_general | solution.py:20
  713.1 1.3 copy.87
  714.4 1.6 collective-permute-start
  716.0 37.2 %collective-permute-done = bf16[2,2,1024,2,128]{4,2,3,1,0:T(8,128)(2,1)S(1)} collective-permute-done((bf16[2,2,1024,2,128]{4,2,3,1,0:T(8,128)(2,1)}, bf16[2,2,1024,2,128]{4,2,3,1,0:T(8,128)(2,1)S(1)}, u32[]{:S(2)}, u32[]{:S(2)}) %collective-permute-start) | collective-permute-done | bytes 2097184 | tf_op jit(solution)/shard_map/while/body/eval_jaxpr/ppermute | solution.py:68
  753.2 77.1 %conditional.2 = (f32[2,4,1024]{2,1,0:T(4,128)}, f32[2,4,1024]{2,1,0:T(4,128)S(1)}, f32[2,4,1024,128]{3,2,1,0:T(8,128)}, f32[2,4,1024]{2,1,0:T(4,128)}, f32[2,4,...) conditional(s32[]{:T(128)} %convert_element_type.81, (bf16[2,2,1024,2,128]{4,2,3,1,0:T(8,128)(2,1)S(1)}, ...), branch_computations={%region_5.7_spmd, %region_8.12_spmd} | conditional | flops 8728379392 | bytes 233766992 | solution.py:70
  754.4 25.8 %bitcast_reduce_fusion = (f32[2,4,1024]{2,1,0:T(4,128)S(1)}, f32[2,2048,1024,4]{2,1,3,0:T(8,128)}) fusion(bf16[2048,2,128,1]{2,0,3,1:T(8,128)(2,1)} %bitcast.165, bf16[1024,2,4,128]{3,0,2,1:T(8,128)(2,1)} %get-tuple-element.326), kind=kOutput, calls=%fused_computation.1 | convolution fusion | flops 4328513536 | bytes 70287360 | tf_op jit(solution)/shard_map/while/body/eval_jaxpr/cond/branch_0_fun/qhge,khe->hgqk/dot_general | solution.py:10
  780.8 21.4 %fusion.2 = f32[2,4,1024]{2,1,0:T(4,128)S(1)} fusion(f32[2,2048,1024,4]{2,1,3,0:T(8,128)} %get-tuple-element.414, f32[2,4,1024]{2,1,0:T(4,128)} %max.6), kind=kLoop, calls=%fused_computation.4 | loop fusion | flops 50323456 | bytes 67174400 | tf_op jit(solution)/shard_map/while/body/eval_jaxpr/cond/branch_0_fun/reduce_sum | solution.py:19
  803.0 27.3 %multiply_add_fusion = f32[2,4,1024,128]{3,2,1,0:T(8,128)} fusion(f32[2,4,1024,128]{3,2,1,0:T(8,128)} %get-tuple-element.328, bf16[2048,2,128,1]{2,0,3,1:T(8,128)(2,1)S(1)} %bitcast.164, f32[2,2048,1024,4]{2,1,3,0:T(8,128)} %get-tuple-element.414, f32[2,4,1024]{2,1,0:T(4,128)} %max.6, f32[2,4,1024]{2,1,0:T(4,128)S(1)} %bitcast.168), kind=kOutput, calls=%fused_computation.6 | convolution fusion | flops 4347396096 | bytes 76611584 | tf_op jit(solution)/shard_map/while/body/eval_jaxpr/cond/branch_0_fun/hgqk,khe->hgqe/dot_general | solution.py:20
  831.1 1.3 copy.87
  832.6 3.0 fusion.55
  836.1 1.3 fusion.54
  838.2 1.4 slice-done
  839.6 1.4 slice-done.1
  841.0 21.8 %convolution_bitcast_fusion = f32[2048,4096]{1,0:T(8,128)} fusion(bf16[2048,128,4,2]{1,0,3,2:T(8,128)(2,1)S(1)} %bitcast.178, bf16[2,4,128,4096]{3,2,1,0:T(8,128)(2,1)S(1)} %bitcast.192), kind=kOutput, calls=%fused_computation.56 | convolution fusion | flops 17179869184 | bytes 46137344 | tf_op jit(solution)/shard_map/hgsqe,hged->sqd/dot_general | solution.py:80
  862.8 561.1 %reduce-scatter.2.cloned.1.call-done = f32[512,4096]{1,0:T(8,128)} async-done(((f32[2048,4096]{1,0:T(8,128)}), f32[512,4096]{1,0:T(8,128)}) %reduce-scatter.2.cloned.1.call-update) | async-done | bytes 8388624 | tf_op jit(solution)/shard_map/reduce_scatter | solution.py:81
  1423.9 6.0 convert_element_type.50
  (40 shorter events, 14.3 us)
Async XLA Ops:
  6.5 292.9 %copy-start = (bf16[4096,256]{1,0:T(8,128)(2,1)S(1)}, bf16[4096,256]{1,0:T(8,128)(2,1)}, u32[]{:S(2)}) copy-start(bf16[4096,256]{1,0:T(8,128)(2,1)} %param.12) | copy-start | bytes 6291460
  6.5 292.9 %all-gather.2.cloned.1.call-start = ((), (), s32[]{:S(2)}) async-start(), calls=%async_computation.1 | async-start | bytes 20971520 | tf_op jit(solution)/shard_map/all_gather | solution.py:32
  7.3 1416.7 %reduce-scatter.2.cloned.1.call-start = ((), (), s32[]{:S(2)}) async-start(), calls=%async_computation.2 | async-start | bytes 41943040 | tf_op jit(solution)/shard_map/reduce_scatter | solution.py:81
  324.2 2.5 copy-start.6
  369.3 19.1 %copy-start.4 = (pred[1024,2048]{0,1:T(8,128)(4,1)S(1)}, pred[1024,2048]{0,1:T(8,128)(4,1)}, u32[]{:S(2)}) copy-start(pred[1024,2048]{0,1:T(8,128)(4,1)} %broadcast_compare_fusion) | copy-start | bytes 6291460
  460.2 28.6 %copy-start.5 = (bf16[1,2,1024,2,128]{4,2,3,1,0:T(8,128)(2,1)S(1)}, bf16[1,2,1024,2,128]{4,2,3,1,0:T(8,128)(2,1)}, u32[]{:S(2)}) copy-start(bf16[1,2,1024,2,128]{4,2,3,1,0:T(8,128)(2,1)} %copy.19) | copy-start | bytes 3145732
  491.7 25.5 %collective-permute-start = (bf16[2,2,1024,2,128]{4,2,3,1,0:T(8,128)(2,1)}, bf16[2,2,1024,2,128]{4,2,3,1,0:T(8,128)(2,1)S(1)}, u32[]{:S(2)}, u32[]{:S(2)}) collective-permute-start(bf16[2,2,1024,2,128]{4,2,3,1,0:T(8,128)(2,1)} %get-tuple-element.552), channel_id=1, source_target_pairs={{0,1},{1,2},{2,3},{3,0},{4,5},{5,6},{6,7},{7,4},{8,9},{9,10},{10,1... | collective-permute-start | bytes 6291464 | tf_op jit(solution)/shard_map/while/body/eval_jaxpr/ppermute | solution.py:68
  596.4 38.8 %collective-permute-start = (bf16[2,2,1024,2,128]{4,2,3,1,0:T(8,128)(2,1)}, bf16[2,2,1024,2,128]{4,2,3,1,0:T(8,128)(2,1)S(1)}, u32[]{:S(2)}, u32[]{:S(2)}) collective-permute-start(bf16[2,2,1024,2,128]{4,2,3,1,0:T(8,128)(2,1)} %get-tuple-element.552), channel_id=1, source_target_pairs={{0,1},{1,2},{2,3},{3,0},{4,5},{5,6},{6,7},{7,4},{8,9},{9,10},{10,1... | collective-permute-start | bytes 6291464 | tf_op jit(solution)/shard_map/while/body/eval_jaxpr/ppermute | solution.py:68
  714.4 38.8 %collective-permute-start = (bf16[2,2,1024,2,128]{4,2,3,1,0:T(8,128)(2,1)}, bf16[2,2,1024,2,128]{4,2,3,1,0:T(8,128)(2,1)S(1)}, u32[]{:S(2)}, u32[]{:S(2)}) collective-permute-start(bf16[2,2,1024,2,128]{4,2,3,1,0:T(8,128)(2,1)} %get-tuple-element.552), channel_id=1, source_target_pairs={{0,1},{1,2},{2,3},{3,0},{4,5},{5,6},{6,7},{7,4},{8,9},{9,10},{10,1... | collective-permute-start | bytes 6291464 | tf_op jit(solution)/shard_map/while/body/eval_jaxpr/ppermute | solution.py:68
  832.6 3.5 copy-start.3
  837.4 2.2 slice-start
  837.8 3.2 slice-start.1
  862.8 567.2 %copy-start.1 = (bf16[4096,256]{1,0:T(8,128)(2,1)S(1)}, bf16[4096,256]{1,0:T(8,128)(2,1)}, u32[]{:S(2)}) copy-start(bf16[4096,256]{1,0:T(8,128)(2,1)} %param.12) | copy-start | bytes 6291460
Sparse Core Ops, SparseCore 0:
  8.9 290.5 all-gather.1
  862.9 560.9 reduce-scatter.1
where the time goes:
time: 1450 us; the launch traced here: 1440 us
  waiting for transfers between devices  937 us (65%)
  matrix products  311 us (21%)
  other arithmetic  122 us (8%)
  local copies, waits for them, and re-layouts  35.9 us (2%)
  starting transfers between devices  16.7 us (1%)
    reduce_scatter x1, waiting for transfers between devices, local_layer(): y_loc = lax.psum_scatter(partial, 'tp', scatter_dimension=0, tiled=True)  561 us
    all_gather x1, waiting for transfers between devices, local_layer(): x_block = lax.all_gather(x_loc, 'tp', axis=0, tiled=True)  289 us
    dot_general x5, matrix products, merge_block(): jnp.einsum('hgqk,khe->hgqe', p_block.astype(jnp.bfloat16), v_part, prefer...  128 us
    dot_general x5, matrix products, block_scores(): jnp.einsum('qhge,khe->hgqk', q_part, k_part, preferred_element_type=jnp.f...  118 us
    reduce_sum x5, other arithmetic, merge_block(): new_sum = run_sum * rescale + p_block.sum(axis=-1)  100 us
    ppermute x3, waiting for transfers between devices, kv_step(): kv_held = lax.ppermute(kv_held, 'cp', shift_pairs)  86.5 us
  transfers between devices with their start and end apart: 5, of which 5 were waited for; matrix products, arithmetic and copies ran while one was open for 0% of the time, Pallas kernels for 0%

commit v1 on v0

v1 whole, which is shorter than its diff:
```python
import functools

import jax
import jax.numpy as jnp
from jax import lax
from jax.experimental import pallas as pl
from jax.experimental.pallas import tpu as pltpu
from jax.sharding import PartitionSpec as P

D = 128
LOG2E = 1.4426950408889634


def flash_kernel(pos_ref, q_ref, k_ref, vt_ref, o_ref, m_ref, l_ref, acc_ref, *, bq, bk, group):
    c = LOG2E * D ** -0.5
    qpos = pos_ref[pl.program_id(1)]

    def tile(kstart, size, mode):
        k = k_ref[pl.ds(kstart, size), :]
        vt = vt_ref[:, pl.ds(kstart, size)]
        for g in range(group):
            q = q_ref[:, g * D:(g + 1) * D]
            s = lax.dot_general(k, q, (((1,), (1,)), ((), ())), preferred_element_type=jnp.float32)
            if mode == "diag":
                ki = lax.broadcasted_iota(jnp.int32, (size, bq), 0)
                qi = lax.broadcasted_iota(jnp.int32, (size, bq), 1)
                s = jnp.where(ki <= qi, s, -jnp.inf)
            m_cur = jnp.max(s, axis=0, keepdims=True)
            if mode == "diag":
                m_new = m_cur
            else:
                m_old = m_ref[g]
                m_new = jnp.maximum(m_old, m_cur)
            p = jnp.exp2((s - m_new) * c)
            l_cur = jnp.sum(p, axis=0, keepdims=True)
            pv = jnp.dot(vt, p.astype(jnp.bfloat16), preferred_element_type=jnp.float32)
            if mode == "diag":
                l_ref[g] = l_cur
                acc_ref[g] = pv
            else:
                alpha = jnp.exp2((m_old - m_new) * c)
                l_ref[g] = l_ref[g] * alpha + l_cur
                acc_ref[g] = acc_ref[g] * alpha + pv
            m_ref[g] = m_new

    tile(pl.multiple_of(qpos, bq), bq, "diag")
    nbig = qpos // bk

    @pl.loop(0, nbig)
    def _(i):
        tile(pl.multiple_of(i * bk, bk), bk, "full")

    @pl.loop(0, (qpos - nbig * bk) // bq)
    def _(i):
        tile(pl.multiple_of(nbig * bk + i * bq, bq), bq, "full")

    for g in range(group):
        o = acc_ref[g] / l_ref[g]
        o_ref[:, g * D:(g + 1) * D] = o.T.astype(jnp.bfloat16)


def flash(pos, q, k, vt, *, bq, bk, group):
    rows = q.shape[0]
    keys = k.shape[0]
    nkv = k.shape[1] // D
    return pl.pallas_call(
        functools.partial(flash_kernel, bq=bq, bk=bk, group=group),
        out_shape=jax.ShapeDtypeStruct((rows, nkv * group * D), jnp.bfloat16),
        grid_spec=pltpu.PrefetchScalarGridSpec(
            num_scalar_prefetch=1,
            grid=(nkv, rows // bq),
            in_specs=[
                pl.BlockSpec((bq, group * D), lambda h, i, pos: (i, h)),
                pl.BlockSpec((keys, D), lambda h, i, pos: (0, h)),
                pl.BlockSpec((D, keys), lambda h, i, pos: (h, 0)),
            ],
            out_specs=pl.BlockSpec((bq, group * D), lambda h, i, pos: (i, h)),
            scratch_shapes=[
                pltpu.VMEM((group, 1, bq), jnp.float32),
                pltpu.VMEM((group, 1, bq), jnp.float32),
                pltpu.VMEM((group, D, bq), jnp.float32),
            ],
        ),
        compiler_params=pltpu.CompilerParams(vmem_limit_bytes=56 * 1024 * 1024),
        cost_estimate=pl.CostEstimate(flops=70_000_000_000, bytes_accessed=32 * 1024 * 1024, transcendentals=67_000_000),
    )(pos, q, k, vt)


def out_kernel(o_ref, w_ref, y_ref):
    y_ref[...] = jnp.dot(o_ref[...], w_ref[0], preferred_element_type=jnp.float32).astype(jnp.bfloat16)


def out_proj(o, w):
    rows, depth = o.shape
    parts, _, cols = w.shape
    return pl.pallas_call(
        out_kernel,
        out_shape=jax.ShapeDtypeStruct((rows, parts * cols), jnp.bfloat16),
        grid=(parts,),
        in_specs=[pl.BlockSpec((rows, depth), lambda i: (0, 0)), pl.BlockSpec((1, depth, cols), lambda i: (i, 0, 0))],
        out_specs=pl.BlockSpec((rows, cols), lambda i: (0, i)),
        compiler_params=pltpu.CompilerParams(vmem_limit_bytes=48 * 1024 * 1024),
        cost_estimate=pl.CostEstimate(flops=2 * rows * depth * parts * cols, bytes_accessed=2 * depth * parts * cols, transcendentals=0),
    )(o, w)


def solution(mesh):
    cp_size = mesh.shape["cp"]
    dp_size = mesh.shape["dp"]
    row_spec = P(("dp", "cp", "tp"), None)

    def local_layer(x_loc, w_q, w_k, w_v, w_o):
        group = w_q.shape[1] // w_k.shape[1]
        parts = dp_size * cp_size
        cols = w_o.shape[1] // parts
        part = lax.axis_index("dp") * cp_size + lax.axis_index("cp")
        x_block = lax.all_gather(x_loc, "tp", axis=0, tiled=True)
        piece_len = x_block.shape[0] // 2
        k_all = jnp.dot(x_block, w_k, preferred_element_type=jnp.float32).astype(jnp.bfloat16)
        vt_all = lax.dot_general(w_v, x_block, (((0,), (1,)), ((), ())), preferred_element_type=jnp.float32).astype(jnp.bfloat16)
        k_g = lax.all_gather(k_all, "cp", axis=0).reshape(cp_size, 2, piece_len, -1)
        vt_g = lax.all_gather(vt_all, "cp", axis=0).reshape(cp_size, -1, 2, piece_len)
        q_all = jnp.dot(x_block, w_q, preferred_element_type=jnp.float32).astype(jnp.bfloat16)
        w_part = lax.dynamic_slice_in_dim(w_o, part * cols, cols, axis=1)
        w_part = lax.all_gather(w_part, "tp", axis=0, tiled=True)
        w_full = lax.all_gather(w_part, ("dp", "cp"), axis=0)
        k_pos = jnp.concatenate([k_g[:, 0], k_g[::-1, 1]]).reshape(2 * cp_size * piece_len, -1)
        vt_pos = jnp.concatenate([vt_g[:, :, 0], vt_g[::-1, :, 1]]).transpose(1, 0, 2).reshape(-1, 2 * cp_size * piece_len)
        bq = 512
        rank = lax.axis_index("cp")
        steps = jnp.arange(piece_len // bq, dtype=jnp.int32) * bq
        pos = jnp.concatenate([rank * piece_len + steps, (2 * cp_size - 1 - rank) * piece_len + steps]).astype(jnp.int32)
        o = flash(pos, q_all, k_pos, vt_pos, bq=bq, bk=1024, group=group)
        o_rows = lax.all_to_all(o, "tp", split_axis=0, concat_axis=1, tiled=True)
        return out_proj(o_rows, w_full)

    return jax.shard_map(local_layer, mesh=mesh, in_specs=(row_spec, P(None, "tp"), P(None, "tp"), P(None, "tp"), P("tp", None)), out_specs=row_spec, check_vma=False)
```

time: 1450 us -> 737 us (0.51)
  waiting for transfers between devices: 937 us -> 359 us
  matrix products: 311 us -> 45 us
  Pallas kernels: 0 us -> 158 us
  other arithmetic: 122 us -> 5.29 us
  blocking collectives: 0 us -> 106 us
  starting transfers between devices: 16.7 us -> 0.35 us
    reduce_scatter x1 -> x0, waiting for transfers between devices: 561 us -> none  [local_layer(): y_loc = lax.psum_scatter(partial, 'tp', scatter_dimension=0, tiled=True)]
    dot_general x12 -> x1, matrix products: 277 us -> 9.29 us  [local_layer(): lax.dot_general(w_v, x_block, (((0,), (1,)), ((), ())), preferred_element...]
    pallas_call x0 -> x2, Pallas kernels: none -> 158 us  [the longest x1 136 us: flash(): pl.pallas_call(functools.partial(flash_kernel, bq=bq, bk=bk, group=group)...]
    all_to_all x0 -> x1, blocking collectives: none -> 106 us  [local_layer(): o_rows = lax.all_to_all(o, 'tp', split_axis=0, concat_axis=1, tiled=True)]
    reduce_sum x5 -> x0, other arithmetic: 100 us -> none  [merge_block(): new_sum = run_sum * rescale + p_block.sum(axis=-1)]
    ppermute x3 -> x0, waiting for transfers between devices: 86.5 us -> none  [kv_step(): kv_held = lax.ppermute(kv_held, 'cp', shift_pairs)]
    all_gather x0 -> x4, waiting for transfers between devices: none -> 68.6 us  [the longest x1 58.2 us: local_layer(): w_part = lax.all_gather(w_part, 'tp', axis=0, tiled=True)]
    ppermute x3 -> x0, starting transfers between devices: 16.7 us -> none  [kv_step(): kv_held = lax.ppermute(kv_held, 'cp', shift_pairs)]
  transfers between devices with their start and end apart: 5 -> 5, of which waited for: 5 -> 3; matrix products, arithmetic and copies ran while one was open for 0% -> 13% of each run, Pallas kernels for 0% -> 19%
where the time goes in v1:
time: 737 us; the launch traced here: 736 us
  waiting for transfers between devices  359 us (49%)
  Pallas kernels  158 us (21%)
  blocking collectives  106 us (14%)
  local copies, waits for them, and re-layouts  48.8 us (7%)
  matrix products  45 us (6%)
  between operations  13.2 us (2%)
    all_gather x1, waiting for transfers between devices, local_layer(): x_block = lax.all_gather(x_loc, 'tp', axis=0, tiled=True)  290 us
    pallas_call x1, Pallas kernels, flash(): pl.pallas_call(functools.partial(flash_kernel, bq=bq, bk=bk, group=group)...  136 us
    all_to_all x1, blocking collectives, local_layer(): o_rows = lax.all_to_all(o, 'tp', split_axis=0, concat_axis=1, tiled=True)  106 us
    all_gather x1, waiting for transfers between devices, local_layer(): w_part = lax.all_gather(w_part, 'tp', axis=0, tiled=True)  58.2 us
    dot_general x1, matrix products, local_layer(): jnp.dot(x_block, w_q, preferred_element_type=jnp.float32)  23.6 us
    pallas_call x1, Pallas kernels, out_proj(): pl.pallas_call(out_kernel, out_shape=jax.ShapeDtypeStruct((rows, parts *...  21.9 us
    unnamed x11, local copies, waits for them, and re-layouts  16.3 us
  transfers between devices with their start and end apart: 5, of which 3 were waited for; matrix products, arithmetic and copies ran while one was open for 13% of the time, Pallas kernels for 19%

profile of v1, /device:TPU:0, one launch (start us, length us, event | category | flops | bytes accessed | tf_op | source)
XLA Modules:
  0.0 736.2 jit_solution(10144855441254819369)
XLA Ops:
  6.5 0.0 copy-start
  6.5 0.0 all-gather.9.cloned.1.call-start
  6.5 0.7 all-gather.9.cloned.1.call-update
  7.3 0.0 all-gather.11.cloned.1.call-start
  7.3 2.3 constant_dynamic-slice_fusion
  9.6 0.0 all-gather.11.cloned.1.call-update
  9.6 0.0 all-gather.15.cloned.1.call-start
  9.7 289.8 %all-gather.9.cloned.1.call-done = bf16[2048,4096]{1,0:T(8,128)(2,1)} async-done(((bf16[512,4096]{1,0:T(8,128)(2,1)}), bf16[2048,4096]{1,0:T(8,128)(2,1)}) %all-gather.9.cloned.1.call-update) | async-done | bytes 16777232 | tf_op jit(solution)/shard_map/all_gather | solution.py:117
  299.5 0.0 copy-done
  299.5 9.3 %convolution_convert_fusion.1 = bf16[256,2048]{1,0:T(8,128)(2,1)} fusion(bf16[4096,256]{1,0:T(8,128)(2,1)S(1)} %copy-done, bf16[2048,4096]{1,0:T(8,128)(2,1)} %all-gather.9.cloned.1.call-done), kind=kOutput, calls=%fused_computation.3 | convolution fusion | flops 4295491584 | bytes 19922944 | tf_op jit(solution)/shard_map/dot_general | solution.py:120
  308.7 0.0 all-gather.15.cloned.1.call-update
  308.8 0.0 all-gather.13.cloned.1.call-start
  308.8 12.1 %convolution_convert_fusion.2 = bf16[2048,256]{1,0:T(8,128)(2,1)} fusion(bf16[2048,4096]{1,0:T(8,128)(2,1)} %all-gather.9.cloned.1.call-done, bf16[4096,256]{1,0:T(8,128)(2,1)} %param.7), kind=kOutput, calls=%fused_computation.4 | convolution fusion | flops 4295491584 | bytes 19922944 | tf_op jit(solution)/shard_map/dot_general | solution.py:119
  320.9 0.0 all-gather.13.cloned.1.call-update
  320.9 0.2 all-gather.17.cloned.1.call-start
  321.1 58.2 %all-gather.11.cloned.1.call-done = bf16[4096,512]{1,0:T(8,128)(2,1)} async-done(((bf16[1024,512]{1,0:T(8,128)(2,1)}), bf16[4096,512]{1,0:T(8,128)(2,1)}) %all-gather.11.cloned.1.call-update) | async-done | bytes 4194320 | tf_op jit(solution)/shard_map/all_gather | solution.py:125
  379.4 0.0 all-gather.17.cloned.1.call-update
  379.4 0.6 pad_add_fusion.pos_ref
  380.0 23.6 %convolution_convert_fusion.q_ref = bf16[2048,1024]{1,0:T(8,128)(2,1)} fusion(bf16[2048,4096]{1,0:T(8,128)(2,1)} %all-gather.9.cloned.1.call-done, bf16[4096,1024]{1,0:T(8,128)(2,1)} %param.6), kind=kOutput, calls=%fused_computation.2 | convolution fusion | flops 17181966336 | bytes 29360128 | tf_op jit(solution)/shard_map/dot_general | solution.py:123
  403.6 10.4 %all-gather.15.cloned.1.call-done = bf16[1024,2048]{1,0:T(8,128)(2,1)} async-done(((bf16[256,2048]{1,0:T(8,128)(2,1)}), bf16[1024,2048]{1,0:T(8,128)(2,1)}) %all-gather.15.cloned.1.call-update) | async-done | bytes 4194320 | tf_op jit(solution)/shard_map/all_gather | solution.py:122
  414.0 7.8 %reshape.17 = bf16[4,256,2,1024]{3,2,1,0:T(2,128)(2,1)} reshape(bf16[1024,2048]{1,0:T(8,128)(2,1)} %all-gather.15.cloned.1.call-done) | data formatting | bytes 8388608 | tf_op jit(solution)/shard_map/reshape | solution.py:122
  421.8 9.8 %fusion.2 = (bf16[4,256,1,1024]{3,2,1,0:T(2,128)(2,1)}, bf16[4,256,1,1024]{3,2,1,0:T(2,128)(2,1)S(1)}) fusion(bf16[4,256,2,1024]{3,2,1,0:T(2,128)(2,1)} %reshape.17), kind=kLoop, calls=%fused_computation.14 | loop fusion | bytes 8388608 | tf_op jit(solution)/shard_map/slice | solution.py:128
  431.5 2.7 copy.19
  434.2 7.6 %rev.7 = bf16[4,256,1,1024]{3,0,1,2:T(4,128)(2,1)} reverse(bf16[4,256,1,1024]{3,0,1,2:T(4,128)(2,1)S(1)} %copy.19), dimensions={0} | reverse | bytes 4194304 | tf_op jit(solution)/shard_map/rev | solution.py:128
  441.8 0.0 copy-start.3
  441.8 5.0 copy.23
  446.8 0.0 copy-done.3
  446.8 2.3 pad_maximum_fusion.1
  449.2 6.4 copy.21
  455.6 0.0 all-gather.13.cloned.1.call-done
  455.6 2.5 slice_bitcast_fusion.1
  458.1 0.1 reverse_bitcast_fusion
  458.2 2.3 pad_maximum_fusion
  460.6 136.3 %shard_map.55 = bf16[2048,1024]{1,0:T(8,128)(2,1)} custom-call(s32[4]{0:T(128)} %pad_add_fusion.pos_ref, bf16[2048,1024]{1,0:T(8,128)(2,1)} %convolution_convert_fusion.q_ref, bf16[8192,256]{1,0:T(8,128)(2,1)} %bitcast.35, bf16[256,8192]{1,0:T(8,128)(2,1)} %bitcast.34), custom_call_target="tpu_custom_call" | custom-call | flops 70000001024 | bytes 33554432 | tf_op jit(solution)/shard_map/pallas_call | solution.py:66
  596.9 106.1 %all_to_all.19 = bf16[4,512,1024]{2,1,0:T(8,128)(2,1)S(1)} all-to-all(bf16[4,512,1024]{2,1,0:T(8,128)(2,1)} %bitcast.36), channel_id=1, replica_groups=mesh['dp'=2,'tp'=4,'cp'=4] {'tp'}, dimensions={0} | all-to-all | bytes 8388608 | tf_op jit(solution)/shard_map/all_to_all | solution.py:134
  703.1 2.5 copy.20
  705.5 0.0 all-gather.17.cloned.1.call-done
  705.5 0.0 copy-start.2
  705.5 2.2 copy-done.2
  707.7 0.0 copy-start.1
  707.7 21.9 %shard_map.56 = bf16[512,4096]{1,0:T(8,128)(2,1)} custom-call(bf16[512,4096]{1,0:T(8,128)(2,1)S(1)} %bitcast.28, bf16[8,4096,512]{2,1,0:T(8,128)(2,1)} %bitcast.37), custom_call_target="tpu_custom_call" | custom-call | flops 17179869184 | bytes 33554432 | tf_op jit(solution)/shard_map/pallas_call | solution.py:96
  729.7 0.0 copy-done.1
  (1 shorter events, 0.0 us)
Async XLA Ops:
  6.5 292.9 %copy-start = (bf16[4096,256]{1,0:T(8,128)(2,1)S(1)}, bf16[4096,256]{1,0:T(8,128)(2,1)}, u32[]{:S(2)}) copy-start(bf16[4096,256]{1,0:T(8,128)(2,1)} %param.8) | copy-start | bytes 6291460
  6.5 292.9 %all-gather.9.cloned.1.call-start = ((), (), s32[]{:S(2)}) async-start(), calls=%async_computation.1 | async-start | bytes 20971520 | tf_op jit(solution)/shard_map/all_gather | solution.py:117
  7.3 372.1 %all-gather.11.cloned.1.call-start = ((), (), s32[]{:S(2)}) async-start(), calls=%async_computation.2 | async-start | bytes 5242880 | tf_op jit(solution)/shard_map/all_gather | solution.py:125
  9.6 404.4 %all-gather.15.cloned.1.call-start = ((), (), s32[]{:S(2)}) async-start(), calls=%async_computation.4 | async-start | bytes 5242880 | tf_op jit(solution)/shard_map/all_gather | solution.py:122
  308.8 146.8 %all-gather.13.cloned.1.call-start = ((), (), s32[]{:S(2)}) async-start(), calls=%async_computation.3 | async-start | bytes 5242880 | tf_op jit(solution)/shard_map/all_gather | solution.py:121
  320.9 384.6 %all-gather.17.cloned.1.call-start = ((), (), s32[]{:S(2)}) async-start(), calls=%async_computation.5 | async-start | bytes 37748736 | tf_op jit(solution)/shard_map/all_gather | solution.py:126
  441.8 5.0 copy-start.3
  705.5 2.2 copy-start.2
  707.7 21.9 %copy-start.1 = (bf16[4096,256]{1,0:T(8,128)(2,1)S(1)}, bf16[4096,256]{1,0:T(8,128)(2,1)}, u32[]{:S(2)}) copy-start(bf16[4096,256]{1,0:T(8,128)(2,1)} %param.8) | copy-start | bytes 6291460
Sparse Core Ops, SparseCore 0:
  8.9 290.5 all-gather.8
  301.0 78.3 all-gather.10
  380.9 33.0 all-gather.14
  415.4 34.2 all-gather.12
  451.5 160.7 all-gather.16

commit v2 on v1

v2 whole, which is shorter than its diff:
```python
import functools

import jax
import jax.numpy as jnp
from jax import lax
from jax.experimental import pallas as pl
from jax.experimental.pallas import tpu as pltpu
from jax.sharding import PartitionSpec as P


D = 128
T = 512
WIDTH = 2
LOG2E = 1.4426950408889634


def flash_kernel(q_ref, *refs, group, cp_size, nkv, head):
    tiles = 4 * cp_size
    kv_in, (o_ref, kv_ref, m_ref, l_ref, acc_ref, s_ref, sems) = refs[:tiles], refs[tiles:]
    c = LOG2E * D ** -0.5
    z = lax.axis_index("tp")
    r = lax.axis_index("cp")
    h = pl.program_id(0)

    def flip(v, bit):
        return v + bit - 2 * bit * ((v // bit) % 2)

    def seq_tile(far, core, row, near):
        src_z, src_r = z, r
        for on, bit in ((far, 2), (near, 1)):
            src_z = flip(src_z, bit) if on else src_z
        for on, bit in ((row, 2), (core, 1)):
            src_r = flip(src_r, bit) if on else src_r
        piece = jnp.where(src_z < 2, src_r, 2 * cp_size - 1 - src_r)
        return 2 * piece + src_z % 2

    slot = pl.program_id(1)
    qt = jnp.where(slot == 0, seq_tile(1, 0, 0, 0), seq_tile(0, 0, 0, 0))

    @pl.when((h == 0) & (slot == 0))
    def _():
        copies = []
        for j in range(tiles):
            pos = seq_tile(j // 8, j // 4 % 2, j // 2 % 2, j % 2)
            copies.append(pltpu.make_async_copy(kv_in[j], kv_ref.at[pos], sems.at[j]))
        for copy in copies:
            copy.start()
        for copy in copies:
            copy.wait()

    k_cols = pl.ds(pl.multiple_of((head + h) * D, D), D)
    v_cols = pl.ds(pl.multiple_of((nkv + head + h) * D, D), D)

    def step(ts, diag):
        ks = [kv_ref[t, :, k_cols] for t in ts]
        vs = [kv_ref[t, :, v_cols] for t in ts]

        def front(g):
            q = q_ref[:, g * D:(g + 1) * D]
            ss = [lax.dot_general(k, q, (((1,), (1,)), ((), ())), preferred_element_type=jnp.float32) for k in ks]
            if diag:
                ki = lax.broadcasted_iota(jnp.int32, (T, T), 0)
                qi = lax.broadcasted_iota(jnp.int32, (T, T), 1)
                ss = [jnp.where(ki <= qi, ss[0], -jnp.inf)]
            for j, s in enumerate(ss):
                s_ref[g % 2, j] = s
            return functools.reduce(jnp.maximum, [jnp.max(s, axis=0, keepdims=True) for s in ss])

        def back(g, m_new):
            if not diag:
                m_old = m_ref[g]
                m_new = jnp.maximum(m_old, m_new)
            ps = [jnp.exp2((s_ref[g % 2, j] - m_new) * c) for j in range(len(ts))]
            l_cur = functools.reduce(jnp.add, [jnp.sum(p, axis=0, keepdims=True) for p in ps])
            pv = functools.reduce(jnp.add, [
                lax.dot_general(v, p.astype(jnp.bfloat16), (((0,), (0,)), ((), ())), preferred_element_type=jnp.float32)
                for v, p in zip(vs, ps)])
            if diag:
                l_ref[g] = l_cur
                acc_ref[g] = pv
            else:
                alpha = jnp.exp2((m_old - m_new) * c)
                l_ref[g] = l_ref[g] * alpha + l_cur
                acc_ref[g] = acc_ref[g] * alpha + pv
            m_ref[g] = m_new

        m_cur = front(0)
        for g in range(group):
            m_nxt = front(g + 1) if g + 1 < group else None
            back(g, m_cur)
            m_cur = m_nxt

    step([qt], True)

    @pl.loop(0, qt // WIDTH)
    def _(i):
        step([WIDTH * i + j for j in range(WIDTH)], False)

    @pl.loop(qt // WIDTH * WIDTH, qt)
    def _(i):
        step([i], False)

    for g in range(group):
        o = acc_ref[g] / l_ref[g]
        o_ref[:, g * D:(g + 1) * D] = o.T.astype(jnp.bfloat16)


def flash(q, tiles, *, group, cp_size, heads=None):
    nkv = tiles[0].shape[1] // (2 * D)
    heads = heads or tuple(range(nkv))
    return pl.pallas_call(
        functools.partial(flash_kernel, group=group, cp_size=cp_size, nkv=nkv, head=heads[0]),
        out_shape=jax.ShapeDtypeStruct((2 * T, len(heads) * group * D), jnp.bfloat16),
        grid=(len(heads), 2),
        in_specs=[pl.BlockSpec((T, group * D), lambda h, i: (i, heads[0] + h))] + [pl.BlockSpec(memory_space=pltpu.HBM)] * len(tiles),
        out_specs=pl.BlockSpec((T, group * D), lambda h, i: (i, h)),
        scratch_shapes=[
            pltpu.VMEM((len(tiles), T, 2 * nkv * D), jnp.bfloat16),
            pltpu.VMEM((group, 1, T), jnp.float32),
            pltpu.VMEM((group, 1, T), jnp.float32),
            pltpu.VMEM((group, D, T), jnp.float32),
            pltpu.VMEM((2, WIDTH, T, T), jnp.float32),
            pltpu.SemaphoreType.DMA((len(tiles),)),
        ],
        compiler_params=pltpu.CompilerParams(vmem_limit_bytes=66_000_000),
        cost_estimate=pl.CostEstimate(flops=20_000_000_000, bytes_accessed=12 * 1024 * 1024, transcendentals=17_000_000),
    )(q, *tiles)


def out_kernel(*refs, counts):
    refs, y_ref = list(refs[:-1]), refs[-1]
    o_groups = [[refs.pop(0) for _ in range(n)] for n in counts]
    acc = None
    for os, w in zip(o_groups, refs):
        start = 0
        for o in os:
            rows = slice(start, start + o.shape[1])
            w_rows = w[rows] if len(w.shape) == 2 else w[0, rows]
            term = jnp.dot(o[...], w_rows, preferred_element_type=jnp.float32)
            acc = term if acc is None else acc + term
            start += o.shape[1]
    y_ref[...] = acc.astype(jnp.bfloat16)


def out_proj(o_groups, ws):
    os = [o for group, _ in o_groups for o in group]
    places = [place for group, place in o_groups for _ in group]
    rows = T
    parts, depth, cols = ws[1].shape
    w_spec = pl.BlockSpec((1, depth, cols), lambda i: (i, 0, 0))
    return pl.pallas_call(
        functools.partial(out_kernel, counts=[len(group) for group, _ in o_groups]),
        out_shape=jax.ShapeDtypeStruct((rows, parts * cols), jnp.bfloat16),
        grid=(parts,),
        in_specs=[pl.BlockSpec((rows, o.shape[1]), lambda i, place=place: (place, 0)) for o, place in zip(os, places)] + [pl.BlockSpec((depth, cols), lambda i: (0, i))] + [w_spec] * 3,
        out_specs=pl.BlockSpec((rows, cols), lambda i: (0, i)),
        compiler_params=pltpu.CompilerParams(vmem_limit_bytes=66_000_000),
        cost_estimate=pl.CostEstimate(flops=8 * rows * depth * parts * cols, bytes_accessed=8 * depth * parts * cols, transcendentals=0),
    )(*os, *ws)


def swap(x, axis, size, bit):
    return lax.ppermute(x, axis, [(i, i ^ bit) for i in range(size)])


def project(x, w):
    return jnp.dot(x, w, preferred_element_type=jnp.float32).astype(jnp.bfloat16)


def after(x, *others):
    return lax.optimization_barrier((x, *others))[0]


def solution(mesh):
    cp_size = mesh.shape["cp"]
    dp_size = mesh.shape["dp"]
    tp_size = mesh.shape["tp"]
    row_spec = P(("dp", "cp", "tp"), None)

    def local_layer(x_own, w_q, w_k, w_v, w_o):
        group = w_q.shape[1] // w_k.shape[1]
        parts = dp_size * cp_size
        part = lax.axis_index("dp") * cp_size + lax.axis_index("cp")

        def own_part(w, axis):
            size = w.shape[axis] // parts
            return lax.dynamic_slice_in_dim(w, part * size, size, axis=axis)

        def tp(x, bit):
            return swap(x, "tp", tp_size, bit)

        def cp(x, bit):
            return swap(x, "cp", cp_size, bit)

        def hops(kv, kv_near):
            first = [kv, kv_near]
            four = first + [cp(t, 2) for t in first]
            return four + [cp(t, 1) for t in four]

        def direct(kv, kv_near):
            tiles = []
            for bits in (0, 2, 1, 3):
                for t in (kv, kv_near):
                    tiles.append(cp(t, bits) if bits else t)
            return tiles

        w_kv = jnp.concatenate([w_k, w_v], axis=1)
        kv_part = tp(jnp.concatenate([own_part(w_k, 0), own_part(w_v, 0)], axis=1), 1)
        q_part = tp(own_part(w_q, 0), 1)
        half = x_own.shape[0] // 2
        x_one = tp(x_own[:half], 2)
        kv_a_own = project(x_own, w_kv)
        w_kv_par = lax.all_gather(after(kv_part, kv_a_own), ("dp", "cp"), axis=0, tiled=True)
        w_q_par = lax.all_gather(after(q_part, kv_a_own), ("dp", "cp"), axis=0, tiled=True)
        a_near = tp(kv_a_own, 1)
        kv_b_own = project(x_own, w_kv_par)
        b_near = tp(kv_b_own, 1)
        q_a_own = project(x_own, w_q)
        q_b_own = project(x_own, w_q_par)

        o_part = own_part(w_o, 1)
        o_near = tp(o_part, 1)

        x_two = tp(after(x_own[half:], x_one, kv_b_own), 2)
        one = [project(x_one, w) for w in (w_kv, w_kv_par, w_q, w_q_par)]
        tiles_a = hops(after(kv_a_own, one[0]), after(b_near, one[0]))
        tiles_b = hops(after(kv_b_own, one[0]), after(a_near, one[0]))
        w_near = lax.all_gather(after(o_near, w_q_par, *tiles_a, *tiles_b), ("dp", "cp"), axis=0)
        x_two = after(x_two, q_a_own, q_b_own, *one, *tiles_a, *tiles_b)

        def far(i, w, own=()):
            return jnp.concatenate([one[i], project(x_two, w), *own])

        kv_a_far = far(0, w_kv)
        kv_b_far = far(1, w_kv_par)
        a_far_near = tp(kv_b_far, 1)
        far_a = hops(kv_a_far, a_far_near)
        b_far_near = tp(kv_a_far, 1)
        far_b = direct(kv_b_far, after(b_far_near, far_a[3]))
        x_two = after(x_two, kv_a_far, kv_b_far)
        q_a = far(2, w_q, [q_a_own])
        q_b = far(3, w_q_par, [q_b_own])
        tiles_a += far_a
        tiles_b += far_b
        o_far = after(tp(after(o_part, a_far_near), 2), *far_a, b_far_near)
        o_cross = tp(o_far, 1)
        w_far = lax.all_gather(o_far, ("dp", "cp"), axis=0)

        def attend(q, prior, tiles, **kw):
            return flash(after(q, *prior), tiles, group=group, cp_size=cp_size, **kw)

        out_a = attend(q_a, [q_b, o_far], tiles_a)
        got_a = tp(out_a[:T], 2)
        w_cross = lax.all_gather(after(o_cross, out_a), ("dp", "cp"), axis=0)
        tiles_b = tiles_b[:8] + [after(t, out_a) for t in tiles_b[8:]]
        out_b, got_b = [out_a], []
        for head in range(w_k.shape[1] // D):
            out_b.append(attend(q_b, out_b[-1:], tiles_b, heads=(head,)))
            got_b.append(tp(out_b[-1][:T], 2))
        return out_proj([([out_a], 1), (out_b[1:], 1), ([got_a], 0), (got_b, 0)], [w_o, w_near, w_far, w_cross])

    return jax.shard_map(local_layer, mesh=mesh, in_specs=(row_spec, P(None, "tp"), P(None, "tp"), P(None, "tp"), P("tp", None)), out_specs=row_spec, check_vma=False)
```

time: 737 us -> 667 us (0.905)
  blocking collectives: 106 us -> 0 us
  waiting for transfers between devices: 359 us -> 396 us
  starting transfers between devices: 0.35 us -> 35.9 us
  Pallas kernels: 158 us -> 124 us
  local copies, waits for them, and re-layouts: 48.8 us -> 24.7 us
  matrix products: 45 us -> 63.1 us
    ppermute x0 -> x38, waiting for transfers between devices: none -> 396 us  [swap(): return lax.ppermute(x, axis, [(i, i ^ bit) for i in range(size)])]
    all_gather x5, waiting for transfers between devices: 358 us -> 0.02 us  [the longest x1 0.01 us: local_layer(): w_cross = lax.all_gather(after(o_cross, out_a), ('dp', 'cp'), axis=0)]
    all_to_all x1 -> x0, blocking collectives: 106 us -> none  [local_layer(): o_rows = lax.all_to_all(o, 'tp', split_axis=0, concat_axis=1, tiled=True)]
    ppermute x0 -> x38, starting transfers between devices: none -> 35.4 us  [swap(): return lax.ppermute(x, axis, [(i, i ^ bit) for i in range(size)])]
    pallas_call x2 -> x4, Pallas kernels: 158 us -> 124 us  [the longest x3 101 us: flash(): pl.pallas_call(functools.partial(flash_kernel, group=group, cp_size=cp_si...]
    dot_general x3 -> x12, matrix products: 45 us -> 63.1 us  [project(): jnp.dot(x, w, preferred_element_type=jnp.float32).astype(jnp.bfloat16)]
    reshape x1 -> x0, local copies, waits for them, and re-layouts: 7.79 us -> none  [local_layer(): lax.all_gather(vt_all, 'cp', axis=0).reshape(cp_size, -1, 2, piece_len)]
    rev x1 -> x0, local copies, waits for them, and re-layouts: 7.57 us -> none  [local_layer(): vt_g[::-1, :, 1]]
  transfers between devices with their start and end apart: 5 -> 43, of which waited for: 3 -> 19; matrix products, arithmetic and copies ran while one was open for 13% -> 12% of each run, Pallas kernels for 19% -> 15%
where the time goes in v2:
time: 667 us; the launch traced here: 661 us
  waiting for transfers between devices  396 us (59%)
  Pallas kernels  124 us (19%)
  matrix products  63.1 us (9%)
  starting transfers between devices  35.9 us (5%)
  local copies, waits for them, and re-layouts  24.7 us (4%)
  between operations  13.8 us (2%)
    ppermute x38, waiting for transfers between devices, swap(): return lax.ppermute(x, axis, [(i, i ^ bit) for i in range(size)])  396 us
    pallas_call x3, Pallas kernels, flash(): pl.pallas_call(functools.partial(flash_kernel, group=group, cp_size=cp_si...  101 us
    dot_general x12, matrix products, project(): jnp.dot(x, w, preferred_element_type=jnp.float32).astype(jnp.bfloat16)  63.1 us
    ppermute x38, starting transfers between devices, swap(): return lax.ppermute(x, axis, [(i, i ^ bit) for i in range(size)])  35.4 us
    pallas_call x1, Pallas kernels, out_proj(): pl.pallas_call(functools.partial(out_kernel, counts=[len(group) for group...  23.4 us
    unnamed x81, local copies, waits for them, and re-layouts  13.6 us
  transfers between devices with their start and end apart: 43, of which 19 were waited for; matrix products, arithmetic and copies ran while one was open for 12% of the time, Pallas kernels for 15%

profile of v2, /device:TPU:0, one launch (start us, length us, event | category | flops | bytes accessed | tf_op | source)
XLA Modules:
  0.0 661.3 jit_solution(13554432559777095050)
XLA Ops:
  7.8 3.1 collective-permute-start.1
  10.9 1.8 constant_dynamic-update-slice_fusion.1
  12.9 3.1 fusion.2.refs_0_
  16.0 6.8 %collective-permute-done.1 = bf16[512,512]{1,0:T(8,128)(2,1)S(1)} collective-permute-done((bf16[512,512]{1,0:T(8,128)(2,1)S(1)}, bf16[512,512]{1,0:T(8,128)(2,1)S(1)}, u32[]{:S(2)}, u32[]{:S(2)}) %collective-permute-start.1) | collective-permute-done | bytes 524320 | tf_op jit(solution)/shard_map/ppermute | solution.py:163
  25.1 1.8 collective-permute-start.3
  26.9 22.6 %collective-permute-done.3 = bf16[512,1024]{1,0:T(8,128)(2,1)S(1)} collective-permute-done((bf16[512,1024]{1,0:T(8,128)(2,1)S(1)}, bf16[512,1024]{1,0:T(8,128)(2,1)S(1)}, u32[]{:S(2)}, u32[]{:S(2)}) %collective-permute-start.3) | collective-permute-done | bytes 1048608 | tf_op jit(solution)/shard_map/ppermute | solution.py:163
  50.5 2.8 fusion.6
  53.3 2.5 collective-permute-start
  55.8 1.6 collective-permute-start.11
  59.2 85.9 %collective-permute-done = bf16[256,4096]{1,0:T(8,128)(2,1)S(1)} collective-permute-done((bf16[256,4096]{1,0:T(8,128)(2,1)S(1)}, bf16[256,4096]{1,0:T(8,128)(2,1)S(1)}, u32[]{:S(2)}, u32[]{:S(2)}) %collective-permute-start) | collective-permute-done | bytes 2097184 | tf_op jit(solution)/shard_map/ppermute | solution.py:163
  147.6 5.8 fusion.3.refs_0_
  155.4 6.2 collective-permute-done.13.refs_3_
  161.6 5.2 collective-permute-done.4.refs_1_
  168.9 2.6 collective-permute-done.5.refs_2_
  172.6 10.0 %collective-permute-done.12.refs_2_ = bf16[512,512]{1,0:T(8,128)(2,1)S(1)} collective-permute-done((bf16[512,512]{1,0:T(8,128)(2,1)}, bf16[512,512]{1,0:T(8,128)(2,1)S(1)}, u32[]{:S(2)}, u32[]{:S(2)}) %collective-permute-start.12) | collective-permute-done | bytes 524320 | tf_op jit(solution)/shard_map/ppermute | solution.py:163
  183.4 10.2 %collective-permute-done.6.refs_3_ = bf16[512,512]{1,0:T(8,128)(2,1)S(1)} collective-permute-done((bf16[512,512]{1,0:T(8,128)(2,1)}, bf16[512,512]{1,0:T(8,128)(2,1)S(1)}, u32[]{:S(2)}, u32[]{:S(2)}) %collective-permute-start.6) | collective-permute-done | bytes 524320 | tf_op jit(solution)/shard_map/ppermute | solution.py:163
  196.5 10.3 %convolution_convert_fusion.1 = bf16[512,1024]{1,0:T(8,128)(2,1)} fusion(bf16[512,4096]{1,0:T(8,128)(2,1)} %param.5, bf16[4096,1024]{1,0:T(8,128)(2,1)} %param.6), kind=kOutput, calls=%fused_computation.3 | convolution fusion | flops 4295491584 | bytes 13631488 | tf_op jit(solution)/shard_map/dot_general | solution.py:167
  206.8 6.7 %convolution_convert_fusion.7 = bf16[256,1024]{1,0:T(8,128)(2,1)} fusion(bf16[256,4096]{1,0:T(8,128)(2,1)S(1)} %copy-done.17, bf16[4096,1024]{1,0:T(8,128)(2,1)} %param.6), kind=kOutput, calls=%fused_computation.10 | convolution fusion | flops 2147745792 | bytes 11010048 | tf_op jit(solution)/shard_map/dot_general | solution.py:167
  213.5 3.0 collective-permute-start.2
  217.8 3.2 fusion.1
  221.0 5.5 fusion
  226.5 81.2 %collective-permute-done.2 = bf16[256,4096]{1,0:T(8,128)(2,1)S(1)} collective-permute-done((bf16[256,4096]{1,0:T(8,128)(2,1)S(1)}, bf16[256,4096]{1,0:T(8,128)(2,1)S(1)}, u32[]{:S(2)}, u32[]{:S(2)}) %collective-permute-start.2) | collective-permute-done | bytes 2097184 | tf_op jit(solution)/shard_map/ppermute | solution.py:163
  309.9 12.5 %convolution_convert_fusion.11 = bf16[256,512]{1,0:T(8,128)(2,1)S(1)} fusion(bf16[256,4096]{1,0:T(8,128)(2,1)S(1)} %collective-permute-done.2, bf16[4096,512]{1,0:T(8,128)(2,1)S(1)} %copy-done.5), kind=kOutput, calls=%fused_computation.17 | convolution fusion | flops 1073872896 | bytes 6553600 | tf_op jit(solution)/shard_map/dot_general | solution.py:167
  323.2 3.4 collective-permute-start.19
  326.6 1.4 collective-permute-start.21
  328.0 9.3 %collective-permute-done.20.refs_10_ = bf16[512,512]{1,0:T(8,128)(2,1)S(1)} collective-permute-done((bf16[512,512]{1,0:T(8,128)(2,1)S(1)}, bf16[512,512]{1,0:T(8,128)(2,1)S(1)}, u32[]{:S(2)}, u32[]{:S(2)}) %collective-permute-start.20) | collective-permute-done | bytes 524320 | tf_op jit(solution)/shard_map/ppermute | solution.py:163
  337.8 9.6 %collective-permute-done.21.refs_11_ = bf16[512,512]{1,0:T(8,128)(2,1)} collective-permute-done((bf16[512,512]{1,0:T(8,128)(2,1)S(1)}, bf16[512,512]{1,0:T(8,128)(2,1)}, u32[]{:S(2)}, u32[]{:S(2)}) %collective-permute-start.21) | collective-permute-done | bytes 524320 | tf_op jit(solution)/shard_map/ppermute | solution.py:163
  347.4 13.5 %collective-permute-done.26.refs_9_ = bf16[512,512]{1,0:T(8,128)(2,1)S(1)} collective-permute-done((bf16[512,512]{1,0:T(8,128)(2,1)S(1)}, bf16[512,512]{1,0:T(8,128)(2,1)S(1)}, u32[]{:S(2)}, u32[]{:S(2)}) %collective-permute-start.26) | collective-permute-done | bytes 524320 | tf_op jit(solution)/shard_map/ppermute | solution.py:163
  362.7 10.2 %collective-permute-done.19 = bf16[1024,512]{1,0:T(8,128)(2,1)} collective-permute-done((bf16[1024,512]{1,0:T(8,128)(2,1)S(1)}, bf16[1024,512]{1,0:T(8,128)(2,1)}, u32[]{:S(2)}, u32[]{:S(2)}) %collective-permute-start.19) | collective-permute-done | bytes 1048608 | tf_op jit(solution)/shard_map/ppermute | solution.py:163
  373.0 6.4 convolution_convert_fusion.5
  379.5 1.6 pad_maximum_fusion.1.q_ref
  382.0 5.9 convolution_convert_fusion.6
  387.9 1.5 pad_maximum_fusion.q_ref
  389.4 47.8 %shard_map.55.refs_0_ = bf16[1024,1024]{1,0:T(8,128)(2,1)} custom-call(bf16[1024,1024]{1,0:T(8,128)(2,1)} %pad_maximum_fusion.q_ref, bf16[512,512]{1,0:T(8,128)(2,1)} %fusion.2.refs_0_, bf16[512,512]{1,0:T(8,128)(2,1)} %copy-done.24, bf16[512,512]{1,0:T(8,128)(2,1)} %collective-permute-done.5.refs_2_, bf16[512,512]{1,0:T(8,128)(2,1)} %copy-done.25, ...), custom_call_target="tpu_custom_call" | custom-call | flops 20000000000 | bytes 12582912 | tf_op jit(solution)/shard_map/pallas_call | solution.py:111
  439.6 1.5 collective-permute-start.28
  441.2 10.5 %collective-permute-done.32.refs_15_ = bf16[512,512]{1,0:T(8,128)(2,1)} collective-permute-done((bf16[512,512]{1,0:T(8,128)(2,1)}, bf16[512,512]{1,0:T(8,128)(2,1)}, u32[]{:S(2)}, u32[]{:S(2)}) %collective-permute-start.32) | collective-permute-done | bytes 524320 | tf_op jit(solution)/shard_map/ppermute | solution.py:163
  451.7 1.4 collective-permute-start.27
  453.2 2.3 slice.20
  455.4 17.2 %collective-permute-done.31.refs_14_ = bf16[512,512]{1,0:T(8,128)(2,1)S(1)} collective-permute-done((bf16[512,512]{1,0:T(8,128)(2,1)S(1)}, bf16[512,512]{1,0:T(8,128)(2,1)S(1)}, u32[]{:S(2)}, u32[]{:S(2)}) %collective-permute-start.31) | collective-permute-done | bytes 524320 | tf_op jit(solution)/shard_map/ppermute | solution.py:163
  473.4 14.1 %collective-permute-done.28.refs_11_ = bf16[512,512]{1,0:T(8,128)(2,1)S(1)} collective-permute-done((bf16[512,512]{1,0:T(8,128)(2,1)}, bf16[512,512]{1,0:T(8,128)(2,1)S(1)}, u32[]{:S(2)}, u32[]{:S(2)}) %collective-permute-start.28) | collective-permute-done | bytes 524320 | tf_op jit(solution)/shard_map/ppermute | solution.py:163
  488.3 21.3 %collective-permute-done.27.refs_10_ = bf16[512,512]{1,0:T(8,128)(2,1)} collective-permute-done((bf16[512,512]{1,0:T(8,128)(2,1)S(1)}, bf16[512,512]{1,0:T(8,128)(2,1)}, u32[]{:S(2)}, u32[]{:S(2)}) %collective-permute-start.27) | collective-permute-done | bytes 524320 | tf_op jit(solution)/shard_map/ppermute | solution.py:163
  509.6 26.5 %shard_map.56.refs_1_ = bf16[1024,512]{1,0:T(8,128)(2,1)} custom-call(bf16[1024,1024]{1,0:T(8,128)(2,1)} %pad_maximum_fusion.1.q_ref, bf16[512,512]{1,0:T(8,128)(2,1)} %copy-done.20, bf16[512,512]{1,0:T(8,128)(2,1)} %collective-permute-done.11.refs_1_, bf16[512,512]{1,0:T(8,128)(2,1)} %copy-done.21, bf16[512,512]{1,0:T(8,128)(2,1)} %collective-permute-done.13.refs_3_, ...), custom_call_target="tpu_custom_call" | custom-call | flops 20000000000 | bytes 12582912 | tf_op jit(solution)/shard_map/pallas_call | solution.py:111
  536.0 3.0 collective-permute-start.33
  539.0 26.5 %shard_map.57.refs_2_ = bf16[1024,512]{1,0:T(8,128)(2,1)} custom-call(bf16[1024,1024]{1,0:T(8,128)(2,1)} %pad_maximum_fusion.1.q_ref, bf16[512,512]{1,0:T(8,128)(2,1)} %copy-done.20, bf16[512,512]{1,0:T(8,128)(2,1)} %collective-permute-done.11.refs_1_, bf16[512,512]{1,0:T(8,128)(2,1)} %copy-done.21, bf16[512,512]{1,0:T(8,128)(2,1)} %collective-permute-done.13.refs_3_, ...), custom_call_target="tpu_custom_call" | custom-call | flops 20000000000 | bytes 12582912 | tf_op jit(solution)/shard_map/pallas_call | solution.py:111
  567.9 2.7 collective-permute-start.34
  570.6 48.8 %collective-permute-done.35.refs_5_ = bf16[512,512]{1,0:T(8,128)(2,1)S(1)} collective-permute-done((bf16[512,512]{1,0:T(8,128)(2,1)S(1)}, bf16[512,512]{1,0:T(8,128)(2,1)S(1)}, u32[]{:S(2)}, u32[]{:S(2)}) %collective-permute-start.35) | collective-permute-done | bytes 524320 | tf_op jit(solution)/shard_map/ppermute | solution.py:163
  619.4 10.8 %collective-permute-done.34.refs_4_ = bf16[512,512]{1,0:T(8,128)(2,1)S(1)} collective-permute-done((bf16[512,512]{1,0:T(8,128)(2,1)S(1)}, bf16[512,512]{1,0:T(8,128)(2,1)S(1)}, u32[]{:S(2)}, u32[]{:S(2)}) %collective-permute-start.34) | collective-permute-done | bytes 524320 | tf_op jit(solution)/shard_map/ppermute | solution.py:163
  631.1 23.4 %shard_map.58 = bf16[512,4096]{1,0:T(8,128)(2,1)} custom-call(bf16[1024,1024]{1,0:T(8,128)(2,1)} %shard_map.55.refs_0_, bf16[1024,512]{1,0:T(8,128)(2,1)} %shard_map.56.refs_1_, bf16[1024,512]{1,0:T(8,128)(2,1)} %shard_map.57.refs_2_, bf16[512,1024]{1,0:T(8,128)(2,1)} %collective-permute-done.33.refs_3_, bf16[512,512]{1,0:T(8,128)(2,1)} %copy-done.39, ...), custom_call_target="tpu_custom_call" | custom-call | flops 17179869184 | bytes 33554432 | tf_op jit(solution)/shard_map/pallas_call | solution.py:151
  (153 shorter events, 32.4 us)
Async XLA Ops:
  6.5 141.1 %all-gather.9.cloned.1.call-start = ((), (), s32[]{:S(2)}) async-start(), calls=%async_computation | async-start | bytes 4718592 | tf_op jit(solution)/shard_map/all_gather | solution.py:213
  7.8 15.0 %collective-permute-start.1 = (bf16[512,512]{1,0:T(8,128)(2,1)S(1)}, bf16[512,512]{1,0:T(8,128)(2,1)S(1)}, u32[]{:S(2)}, u32[]{:S(2)}) collective-permute-start(bf16[512,512]{1,0:T(8,128)(2,1)S(1)} %pad_maximum_fusion.2), channel_id=1, source_target_pairs={{0,4},{4,0},{8,12},{12,8},{1,5},{5,1},{9,13},{13,9},{2,6},{6,2},{1... | collective-permute-start | bytes 1572872 | tf_op jit(solution)/shard_map/ppermute | solution.py:163
  23.7 172.4 %all-gather.11.cloned.1.call-start = ((), (), s32[]{:S(2)}) async-start(), calls=%async_computation.1 | async-start | bytes 9437184 | tf_op jit(solution)/shard_map/all_gather | solution.py:214
  25.1 24.4 %collective-permute-start.3 = (bf16[512,1024]{1,0:T(8,128)(2,1)S(1)}, bf16[512,1024]{1,0:T(8,128)(2,1)S(1)}, u32[]{:S(2)}, u32[]{:S(2)}) collective-permute-start(bf16[512,1024]{1,0:T(8,128)(2,1)S(1)} %constant_dynamic-slice_fusion.1), channel_id=1, source_target_pairs={{0,4},{4,0},{8,12},{12,8},{1,5},{5,1},{9,13},{13,9},{2,6},{6,2},{1... | collective-permute-start | bytes 3145736 | tf_op jit(solution)/shard_map/ppermute | solution.py:163
  50.5 580.6 %all-gather.13.cloned.1.call-start = ((), (), s32[]{:S(2)}) async-start(), calls=%async_computation.2 | async-start | bytes 9437184 | tf_op jit(solution)/shard_map/all_gather | solution.py:228
  50.5 94.6 %copy-start.4 = (bf16[4096,512]{1,0:T(8,128)(2,1)S(1)}, bf16[4096,512]{1,0:T(8,128)(2,1)}, u32[]{:S(2)}) copy-start(bf16[4096,512]{1,0:T(8,128)(2,1)} %copy-done.3) | copy-start | bytes 12582916
  53.3 91.8 %collective-permute-start = (bf16[256,4096]{1,0:T(8,128)(2,1)S(1)}, bf16[256,4096]{1,0:T(8,128)(2,1)S(1)}, u32[]{:S(2)}, u32[]{:S(2)}) collective-permute-start(bf16[256,4096]{1,0:T(8,128)(2,1)S(1)} %get-tuple-element.55), channel_id=1, source_target_pairs={{0,8},{4,12},{8,0},{12,4},{1,9},{5,13},{9,1},{13,5},{2,10},{6,14},... | collective-permute-start | bytes 6291464 | tf_op jit(solution)/shard_map/ppermute | solution.py:163
  55.8 90.6 %collective-permute-start.11 = (bf16[512,512]{1,0:T(8,128)(2,1)}, bf16[512,512]{1,0:T(8,128)(2,1)}, u32[]{:S(2)}, u32[]{:S(2)}) collective-permute-start(bf16[512,512]{1,0:T(8,128)(2,1)} %fusion.2.refs_0_), channel_id=1, source_target_pairs={{0,4},{4,0},{8,12},{12,8},{1,5},{5,1},{9,13},{13,9},{2,6},{6,2},{1... | collective-permute-start | bytes 1572872 | tf_op jit(solution)/shard_map/ppermute | solution.py:163
  58.7 108.9 %collective-permute-start.36 = (bf16[1024,512]{1,0:T(8,128)(2,1)S(1)}, bf16[1024,512]{1,0:T(8,128)(2,1)}, u32[]{:S(2)}, u32[]{:S(2)}) collective-permute-start(bf16[1024,512]{1,0:T(8,128)(2,1)S(1)} %constant_dynamic-slice_fusion), channel_id=1, source_target_pairs={{0,4},{4,0},{8,12},{12,8},{1,5},{5,1},{9,13},{13,9},{2,6},{6,2},{1... | collective-permute-start | bytes 3145736 | tf_op jit(solution)/shard_map/ppermute | solution.py:163
  146.5 15.1 %collective-permute-start.13 = (bf16[512,512]{1,0:T(8,128)(2,1)}, bf16[512,512]{1,0:T(8,128)(2,1)}, u32[]{:S(2)}, u32[]{:S(2)}) collective-permute-start(bf16[512,512]{1,0:T(8,128)(2,1)} %collective-permute-done.11.refs_1_), channel_id=1, source_target_pairs={{0,2},{1,3},{2,0},{3,1},{4,6},{5,7},{6,4},{7,5},{8,10},{9,11},{10,... | collective-permute-start | bytes 1572872 | tf_op jit(solution)/shard_map/ppermute | solution.py:163
  154.2 12.6 %collective-permute-start.4 = (bf16[512,512]{1,0:T(8,128)(2,1)S(1)}, bf16[512,512]{1,0:T(8,128)(2,1)S(1)}, u32[]{:S(2)}, u32[]{:S(2)}) collective-permute-start(bf16[512,512]{1,0:T(8,128)(2,1)S(1)} %fusion.3.refs_0_), channel_id=1, source_target_pairs={{0,4},{4,0},{8,12},{12,8},{1,5},{5,1},{9,13},{13,9},{2,6},{6,2},{1... | collective-permute-start | bytes 1572872 | tf_op jit(solution)/shard_map/ppermute | solution.py:163
  154.9 16.6 %collective-permute-start.5 = (bf16[512,512]{1,0:T(8,128)(2,1)}, bf16[512,512]{1,0:T(8,128)(2,1)}, u32[]{:S(2)}, u32[]{:S(2)}) collective-permute-start(bf16[512,512]{1,0:T(8,128)(2,1)} %fusion.2.refs_0_), channel_id=1, source_target_pairs={{0,2},{1,3},{2,0},{3,1},{4,6},{5,7},{6,4},{7,5},{8,10},{9,11},{10,... | collective-permute-start | bytes 1572872 | tf_op jit(solution)/shard_map/ppermute | solution.py:163
  155.4 16.6 %collective-permute-start.15 = (bf16[512,512]{1,0:T(8,128)(2,1)}, bf16[512,512]{1,0:T(8,128)(2,1)}, u32[]{:S(2)}, u32[]{:S(2)}) collective-permute-start(bf16[512,512]{1,0:T(8,128)(2,1)} %collective-permute-done.11.refs_1_), channel_id=1, source_target_pairs={{0,1},{1,0},{2,3},{3,2},{4,5},{5,4},{6,7},{7,6},{8,9},{9,8},{10,11... | collective-permute-start | bytes 1572872 | tf_op jit(solution)/shard_map/ppermute | solution.py:163
  161.6 10.4 %collective-permute-start.7 = (bf16[512,512]{1,0:T(8,128)(2,1)}, bf16[512,512]{1,0:T(8,128)(2,1)}, u32[]{:S(2)}, u32[]{:S(2)}) collective-permute-start(bf16[512,512]{1,0:T(8,128)(2,1)} %fusion.2.refs_0_), channel_id=1, source_target_pairs={{0,1},{1,0},{2,3},{3,2},{4,5},{5,4},{6,7},{7,6},{8,9},{9,8},{10,11... | collective-permute-start | bytes 1572872 | tf_op jit(solution)/shard_map/ppermute | solution.py:163
  167.6 4.9 collective-permute-start.17
  167.6 15.0 %collective-permute-start.12 = (bf16[512,512]{1,0:T(8,128)(2,1)}, bf16[512,512]{1,0:T(8,128)(2,1)S(1)}, u32[]{:S(2)}, u32[]{:S(2)}) collective-permute-start(bf16[512,512]{1,0:T(8,128)(2,1)} %copy-done.20), channel_id=1, source_target_pairs={{0,2},{1,3},{2,0},{3,1},{4,6},{5,7},{6,4},{7,5},{8,10},{9,11},{10,... | collective-permute-start | bytes 1572872 | tf_op jit(solution)/shard_map/ppermute | solution.py:163
  171.5 22.1 %collective-permute-start.6 = (bf16[512,512]{1,0:T(8,128)(2,1)}, bf16[512,512]{1,0:T(8,128)(2,1)S(1)}, u32[]{:S(2)}, u32[]{:S(2)}) collective-permute-start(bf16[512,512]{1,0:T(8,128)(2,1)} %copy-done.24), channel_id=1, source_target_pairs={{0,2},{1,3},{2,0},{3,1},{4,6},{5,7},{6,4},{7,5},{8,10},{9,11},{10,... | collective-permute-start | bytes 1572872 | tf_op jit(solution)/shard_map/ppermute | solution.py:163
  172.0 21.6 %collective-permute-start.9 = (bf16[512,512]{1,0:T(8,128)(2,1)}, bf16[512,512]{1,0:T(8,128)(2,1)S(1)}, u32[]{:S(2)}, u32[]{:S(2)}) collective-permute-start(bf16[512,512]{1,0:T(8,128)(2,1)} %collective-permute-done.5.refs_2_), channel_id=1, source_target_pairs={{0,1},{1,0},{2,3},{3,2},{4,5},{5,4},{6,7},{7,6},{8,9},{9,8},{10,11... | collective-permute-start | bytes 1572872 | tf_op jit(solution)/shard_map/ppermute | solution.py:163
  172.0 21.6 %collective-permute-start.14 = (bf16[512,512]{1,0:T(8,128)(2,1)}, bf16[512,512]{1,0:T(8,128)(2,1)S(1)}, u32[]{:S(2)}, u32[]{:S(2)}) collective-permute-start(bf16[512,512]{1,0:T(8,128)(2,1)} %copy-done.20), channel_id=1, source_target_pairs={{0,1},{1,0},{2,3},{3,2},{4,5},{5,4},{6,7},{7,6},{8,9},{9,8},{10,11... | collective-permute-start | bytes 1572872 | tf_op jit(solution)/shard_map/ppermute | solution.py:163
  172.5 22.0 %collective-permute-start.8 = (bf16[512,512]{1,0:T(8,128)(2,1)}, bf16[512,512]{1,0:T(8,128)(2,1)S(1)}, u32[]{:S(2)}, u32[]{:S(2)}) collective-permute-start(bf16[512,512]{1,0:T(8,128)(2,1)} %copy-done.24), channel_id=1, source_target_pairs={{0,1},{1,0},{2,3},{3,2},{4,5},{5,4},{6,7},{7,6},{8,9},{9,8},{10,11... | collective-permute-start | bytes 1572872 | tf_op jit(solution)/shard_map/ppermute | solution.py:163
  183.4 10.3 %collective-permute-start.16 = (bf16[512,512]{1,0:T(8,128)(2,1)S(1)}, bf16[512,512]{1,0:T(8,128)(2,1)S(1)}, u32[]{:S(2)}, u32[]{:S(2)}) collective-permute-start(bf16[512,512]{1,0:T(8,128)(2,1)S(1)} %collective-permute-done.12.refs_2_), channel_id=1, source_target_pairs={{0,1},{1,0},{2,3},{3,2},{4,5},{5,4},{6,7},{7,6},{8,9},{9,8},{10,11... | collective-permute-start | bytes 1572872 | tf_op jit(solution)/shard_map/ppermute | solution.py:163
  193.6 2.4 collective-permute-start.10
  196.1 435.0 %all-gather.15.cloned.1.call-start = ((), (), s32[]{:S(2)}) async-start(), calls=%async_computation.3 | async-start | bytes 9437184 | tf_op jit(solution)/shard_map/all_gather | solution.py:247
  213.5 94.3 %collective-permute-start.2 = (bf16[256,4096]{1,0:T(8,128)(2,1)S(1)}, bf16[256,4096]{1,0:T(8,128)(2,1)S(1)}, u32[]{:S(2)}, u32[]{:S(2)}) collective-permute-start(bf16[256,4096]{1,0:T(8,128)(2,1)S(1)} %get-tuple-element.31), channel_id=1, source_target_pairs={{0,8},{4,12},{8,0},{12,4},{1,9},{5,13},{9,1},{13,5},{2,10},{6,14},... | collective-permute-start | bytes 6291464 | tf_op jit(solution)/shard_map/ppermute | solution.py:163
  226.5 83.4 %copy-start.5 = (bf16[4096,512]{1,0:T(8,128)(2,1)S(1)}, bf16[4096,512]{1,0:T(8,128)(2,1)}, u32[]{:S(2)}) copy-start(bf16[4096,512]{1,0:T(8,128)(2,1)} %copy-done.3) | copy-start | bytes 12582916
  309.1 142.6 %copy-start.9 = (bf16[512,512]{1,0:T(8,128)(2,1)}, bf16[512,512]{1,0:T(8,128)(2,1)S(1)}, u32[]{:S(2)}) copy-start(bf16[512,512]{1,0:T(8,128)(2,1)S(1)} %pad_maximum_fusion.4.refs_8_) | copy-start | bytes 1572868
  309.1 14.1 %collective-permute-start.18 = (bf16[512,512]{1,0:T(8,128)(2,1)S(1)}, bf16[512,512]{1,0:T(8,128)(2,1)S(1)}, u32[]{:S(2)}, u32[]{:S(2)}) collective-permute-start(bf16[512,512]{1,0:T(8,128)(2,1)S(1)} %pad_maximum_fusion.4.refs_8_), channel_id=1, source_target_pairs={{0,4},{4,0},{8,12},{12,8},{1,5},{5,1},{9,13},{13,9},{2,6},{6,2},{1... | collective-permute-start | bytes 1572872 | tf_op jit(solution)/shard_map/ppermute | solution.py:163
  322.4 57.1 %copy-start.10 = (bf16[512,512]{1,0:T(8,128)(2,1)}, bf16[512,512]{1,0:T(8,128)(2,1)S(1)}, u32[]{:S(2)}) copy-start(bf16[512,512]{1,0:T(8,128)(2,1)S(1)} %pad_maximum_fusion.3.refs_8_) | copy-start | bytes 1572868
  322.4 14.9 %collective-permute-start.20 = (bf16[512,512]{1,0:T(8,128)(2,1)S(1)}, bf16[512,512]{1,0:T(8,128)(2,1)S(1)}, u32[]{:S(2)}, u32[]{:S(2)}) collective-permute-start(bf16[512,512]{1,0:T(8,128)(2,1)S(1)} %pad_maximum_fusion.3.refs_8_), channel_id=1, source_target_pairs={{0,2},{1,3},{2,0},{3,1},{4,6},{5,7},{6,4},{7,5},{8,10},{9,11},{10,... | collective-permute-start | bytes 1572872 | tf_op jit(solution)/shard_map/ppermute | solution.py:163
  323.2 14.2 %collective-permute-start.22 = (bf16[512,512]{1,0:T(8,128)(2,1)S(1)}, bf16[512,512]{1,0:T(8,128)(2,1)S(1)}, u32[]{:S(2)}, u32[]{:S(2)}) collective-permute-start(bf16[512,512]{1,0:T(8,128)(2,1)S(1)} %pad_maximum_fusion.3.refs_8_), channel_id=1, source_target_pairs={{0,1},{1,0},{2,3},{3,2},{4,5},{5,4},{6,7},{7,6},{8,9},{9,8},{10,11... | collective-permute-start | bytes 1572872 | tf_op jit(solution)/shard_map/ppermute | solution.py:163
  323.2 37.7 %copy-start.29 = (bf16[512,512]{1,0:T(8,128)(2,1)}, bf16[512,512]{1,0:T(8,128)(2,1)S(1)}, u32[]{:S(2)}) copy-start(bf16[512,512]{1,0:T(8,128)(2,1)S(1)} %collective-permute-done.18.refs_9_) | copy-start | bytes 1572868
  323.2 49.8 %collective-permute-start.19 = (bf16[1024,512]{1,0:T(8,128)(2,1)S(1)}, bf16[1024,512]{1,0:T(8,128)(2,1)}, u32[]{:S(2)}, u32[]{:S(2)}) collective-permute-start(bf16[1024,512]{1,0:T(8,128)(2,1)S(1)} %constant_dynamic-slice_fusion), channel_id=1, source_target_pairs={{0,8},{4,12},{8,0},{12,4},{1,9},{5,13},{9,1},{13,5},{2,10},{6,14},... | collective-permute-start | bytes 3145736 | tf_op jit(solution)/shard_map/ppermute | solution.py:163
  326.6 20.8 %collective-permute-start.21 = (bf16[512,512]{1,0:T(8,128)(2,1)S(1)}, bf16[512,512]{1,0:T(8,128)(2,1)}, u32[]{:S(2)}, u32[]{:S(2)}) collective-permute-start(bf16[512,512]{1,0:T(8,128)(2,1)S(1)} %collective-permute-done.18.refs_9_), channel_id=1, source_target_pairs={{0,2},{1,3},{2,0},{3,1},{4,6},{5,7},{6,4},{7,5},{8,10},{9,11},{10,... | collective-permute-start | bytes 1572872 | tf_op jit(solution)/shard_map/ppermute | solution.py:163
  328.0 32.9 %collective-permute-start.26 = (bf16[512,512]{1,0:T(8,128)(2,1)S(1)}, bf16[512,512]{1,0:T(8,128)(2,1)S(1)}, u32[]{:S(2)}, u32[]{:S(2)}) collective-permute-start(bf16[512,512]{1,0:T(8,128)(2,1)S(1)} %pad_maximum_fusion.3.refs_8_), channel_id=1, source_target_pairs={{0,4},{4,0},{8,12},{12,8},{1,5},{5,1},{9,13},{13,9},{2,6},{6,2},{1... | collective-permute-start | bytes 1572872 | tf_op jit(solution)/shard_map/ppermute | solution.py:163
  337.3 23.6 %collective-permute-start.23 = (bf16[512,512]{1,0:T(8,128)(2,1)S(1)}, bf16[512,512]{1,0:T(8,128)(2,1)S(1)}, u32[]{:S(2)}, u32[]{:S(2)}) collective-permute-start(bf16[512,512]{1,0:T(8,128)(2,1)S(1)} %collective-permute-done.18.refs_9_), channel_id=1, source_target_pairs={{0,1},{1,0},{2,3},{3,2},{4,5},{5,4},{6,7},{7,6},{8,9},{9,8},{10,11... | collective-permute-start | bytes 1572872 | tf_op jit(solution)/shard_map/ppermute | solution.py:163
  337.3 23.6 %collective-permute-start.24 = (bf16[512,512]{1,0:T(8,128)(2,1)S(1)}, bf16[512,512]{1,0:T(8,128)(2,1)S(1)}, u32[]{:S(2)}, u32[]{:S(2)}) collective-permute-start(bf16[512,512]{1,0:T(8,128)(2,1)S(1)} %collective-permute-done.20.refs_10_), channel_id=1, source_target_pairs={{0,1},{1,0},{2,3},{3,2},{4,5},{5,4},{6,7},{7,6},{8,9},{9,8},{10,11... | collective-permute-start | bytes 1572872 | tf_op jit(solution)/shard_map/ppermute | solution.py:163
  347.4 25.5 %collective-permute-start.25 = (bf16[512,512]{1,0:T(8,128)(2,1)}, bf16[512,512]{1,0:T(8,128)(2,1)}, u32[]{:S(2)}, u32[]{:S(2)}) collective-permute-start(bf16[512,512]{1,0:T(8,128)(2,1)} %collective-permute-done.21.refs_11_), channel_id=1, source_target_pairs={{0,1},{1,0},{2,3},{3,2},{4,5},{5,4},{6,7},{7,6},{8,9},{9,8},{10,11... | collective-permute-start | bytes 1572872 | tf_op jit(solution)/shard_map/ppermute | solution.py:163
  373.0 258.1 %all-gather.17.cloned.1.call-start = ((), (), s32[]{:S(2)}) async-start(), calls=%async_computation.4 | async-start | bytes 9437184 | tf_op jit(solution)/shard_map/all_gather | solution.py:254
  389.4 47.9 %collective-permute-start.37 = (bf16[1024,512]{1,0:T(8,128)(2,1)}, bf16[1024,512]{1,0:T(8,128)(2,1)}, u32[]{:S(2)}, u32[]{:S(2)}) collective-permute-start(bf16[1024,512]{1,0:T(8,128)(2,1)} %collective-permute-done.19), channel_id=1, source_target_pairs={{0,4},{4,0},{8,12},{12,8},{1,5},{5,1},{9,13},{13,9},{2,6},{6,2},{1... | collective-permute-start | bytes 3145736 | tf_op jit(solution)/shard_map/ppermute | solution.py:163
  437.3 14.4 %collective-permute-start.32 = (bf16[512,512]{1,0:T(8,128)(2,1)}, bf16[512,512]{1,0:T(8,128)(2,1)}, u32[]{:S(2)}, u32[]{:S(2)}) collective-permute-start(bf16[512,512]{1,0:T(8,128)(2,1)} %copy-done.28), channel_id=1, source_target_pairs={{0,3},{1,2},{2,1},{3,0},{4,7},{5,6},{6,5},{7,4},{8,11},{9,10},{10,... | collective-permute-start | bytes 1572872 | tf_op jit(solution)/shard_map/ppermute | solution.py:163
  438.6 33.9 %collective-permute-start.31 = (bf16[512,512]{1,0:T(8,128)(2,1)S(1)}, bf16[512,512]{1,0:T(8,128)(2,1)S(1)}, u32[]{:S(2)}, u32[]{:S(2)}) collective-permute-start(bf16[512,512]{1,0:T(8,128)(2,1)S(1)} %pad_maximum_fusion.4.refs_8_), channel_id=1, source_target_pairs={{0,3},{1,2},{2,1},{3,0},{4,7},{5,6},{6,5},{7,4},{8,11},{9,10},{10,... | collective-permute-start | bytes 1572872 | tf_op jit(solution)/shard_map/ppermute | solution.py:163
  439.1 33.5 %collective-permute-start.30 = (bf16[512,512]{1,0:T(8,128)(2,1)}, bf16[512,512]{1,0:T(8,128)(2,1)S(1)}, u32[]{:S(2)}, u32[]{:S(2)}) collective-permute-start(bf16[512,512]{1,0:T(8,128)(2,1)} %copy-done.28), channel_id=1, source_target_pairs={{0,1},{1,0},{2,3},{3,2},{4,5},{5,4},{6,7},{7,6},{8,9},{9,8},{10,11... | collective-permute-start | bytes 1572872 | tf_op jit(solution)/shard_map/ppermute | solution.py:163
  439.2 33.4 %collective-permute-start.29 = (bf16[512,512]{1,0:T(8,128)(2,1)S(1)}, bf16[512,512]{1,0:T(8,128)(2,1)S(1)}, u32[]{:S(2)}, u32[]{:S(2)}) collective-permute-start(bf16[512,512]{1,0:T(8,128)(2,1)S(1)} %pad_maximum_fusion.4.refs_8_), channel_id=1, source_target_pairs={{0,1},{1,0},{2,3},{3,2},{4,5},{5,4},{6,7},{7,6},{8,9},{9,8},{10,11... | collective-permute-start | bytes 1572872 | tf_op jit(solution)/shard_map/ppermute | solution.py:163
  439.6 47.8 %collective-permute-start.28 = (bf16[512,512]{1,0:T(8,128)(2,1)}, bf16[512,512]{1,0:T(8,128)(2,1)S(1)}, u32[]{:S(2)}, u32[]{:S(2)}) collective-permute-start(bf16[512,512]{1,0:T(8,128)(2,1)} %copy-done.28), channel_id=1, source_target_pairs={{0,2},{1,3},{2,0},{3,1},{4,6},{5,7},{6,4},{7,5},{8,10},{9,11},{10,... | collective-permute-start | bytes 1572872 | tf_op jit(solution)/shard_map/ppermute | solution.py:163
  451.7 57.8 %collective-permute-start.27 = (bf16[512,512]{1,0:T(8,128)(2,1)S(1)}, bf16[512,512]{1,0:T(8,128)(2,1)}, u32[]{:S(2)}, u32[]{:S(2)}) collective-permute-start(bf16[512,512]{1,0:T(8,128)(2,1)S(1)} %pad_maximum_fusion.4.refs_8_), channel_id=1, source_target_pairs={{0,2},{1,3},{2,0},{3,1},{4,6},{5,7},{6,4},{7,5},{8,10},{9,11},{10,... | collective-permute-start | bytes 1572872 | tf_op jit(solution)/shard_map/ppermute | solution.py:163
  536.0 95.0 %collective-permute-start.33 = (bf16[512,1024]{1,0:T(8,128)(2,1)}, bf16[512,1024]{1,0:T(8,128)(2,1)}, u32[]{:S(2)}, u32[]{:S(2)}) collective-permute-start(bf16[512,1024]{1,0:T(8,128)(2,1)} %slice.20), channel_id=1, source_target_pairs={{0,8},{4,12},{8,0},{12,4},{1,9},{5,13},{9,1},{13,5},{2,10},{6,14},... | collective-permute-start | bytes 3145736 | tf_op jit(solution)/shard_map/ppermute | solution.py:163
  567.6 51.8 %collective-permute-start.35 = (bf16[512,512]{1,0:T(8,128)(2,1)S(1)}, bf16[512,512]{1,0:T(8,128)(2,1)S(1)}, u32[]{:S(2)}, u32[]{:S(2)}) collective-permute-start(bf16[512,512]{1,0:T(8,128)(2,1)S(1)} %slice.22), channel_id=1, source_target_pairs={{0,8},{4,12},{8,0},{12,4},{1,9},{5,13},{9,1},{13,5},{2,10},{6,14},... | collective-permute-start | bytes 1572872 | tf_op jit(solution)/shard_map/ppermute | solution.py:163
  567.9 62.3 %collective-permute-start.34 = (bf16[512,512]{1,0:T(8,128)(2,1)S(1)}, bf16[512,512]{1,0:T(8,128)(2,1)S(1)}, u32[]{:S(2)}, u32[]{:S(2)}) collective-permute-start(bf16[512,512]{1,0:T(8,128)(2,1)S(1)} %slice.21), channel_id=1, source_target_pairs={{0,8},{4,12},{8,0},{12,4},{1,9},{5,13},{9,1},{13,5},{2,10},{6,14},... | collective-permute-start | bytes 1572872 | tf_op jit(solution)/shard_map/ppermute | solution.py:163
  (35 other events, 192.3 us)
Sparse Core Ops, SparseCore 0:
  23.8 37.9 all-gather.8
  63.7 54.2 all-gather.10
  196.2 55.7 all-gather.12
  373.1 53.8 all-gather.14
  437.4 83.7 all-gather.16

commit v3 on v2

--- a/solution.py
+++ b/solution.py
@@ -130,7 +130,7 @@
 def out_kernel(*refs, counts):
     refs, y_ref = list(refs[:-1]), refs[-1]
     o_groups = [[refs.pop(0) for _ in range(n)] for n in counts]
-    acc = None
+    acc = refs.pop()[...] if len(refs) > len(counts) else None
     for os, w in zip(o_groups, refs):
         start = 0
         for o in os:
@@ -139,24 +139,27 @@
             term = jnp.dot(o[...], w_rows, preferred_element_type=jnp.float32)
             acc = term if acc is None else acc + term
             start += o.shape[1]
-    y_ref[...] = acc.astype(jnp.bfloat16)
-
-
-def out_proj(o_groups, ws):
+    y_ref[...] = acc.astype(y_ref.dtype)
+
+
+def out_proj(o_groups, ws, dtype, part=None):
     os = [o for group, _ in o_groups for o in group]
     places = [place for group, place in o_groups for _ in group]
     rows = T
-    parts, depth, cols = ws[1].shape
-    w_spec = pl.BlockSpec((1, depth, cols), lambda i: (i, 0, 0))
+    parts, depth, cols = ws[-1].shape
+    own_spec = pl.BlockSpec((depth, cols), lambda i: (0, i))
+    y_spec = pl.BlockSpec((rows, cols), lambda i: (0, i))
     return pl.pallas_call(
         functools.partial(out_kernel, counts=[len(group) for group, _ in o_groups]),
-        out_shape=jax.ShapeDtypeStruct((rows, parts * cols), jnp.bfloat16),
+        out_shape=jax.ShapeDtypeStruct((rows, parts * cols), dtype),
         grid=(parts,),
-        in_specs=[pl.BlockSpec((rows, o.shape[1]), lambda i, place=place: (place, 0)) for o, place in zip(os, places)] + [pl.BlockSpec((depth, cols), lambda i: (0, i))] + [w_spec] * 3,
-        out_specs=pl.BlockSpec((rows, cols), lambda i: (0, i)),
+        in_specs=[pl.BlockSpec((rows, o.shape[1]), lambda i, place=place: (place, 0)) for o, place in zip(os, places)]
+        + [own_spec if w.ndim == 2 else pl.BlockSpec((1, depth, cols), lambda i: (i, 0, 0)) for w in ws]
+        + [y_spec] * (part is not None),
+        out_specs=y_spec,
         compiler_params=pltpu.CompilerParams(vmem_limit_bytes=66_000_000),
-        cost_estimate=pl.CostEstimate(flops=8 * rows * depth * parts * cols, bytes_accessed=8 * depth * parts * cols, transcendentals=0),
-    )(*os, *ws)
+        cost_estimate=pl.CostEstimate(flops=2 * len(ws) * rows * depth * parts * cols, bytes_accessed=2 * len(ws) * depth * parts * cols, transcendentals=0),
+    )(*os, *ws, *([] if part is None else [part]))
 
 
 def swap(x, axis, size, bit):
@@ -196,13 +199,6 @@
             first = [kv, kv_near]
             four = first + [cp(t, 2) for t in first]
             return four + [cp(t, 1) for t in four]
-
-        def direct(kv, kv_near):
-            tiles = []
-            for bits in (0, 2, 1, 3):
-                for t in (kv, kv_near):
-                    tiles.append(cp(t, bits) if bits else t)
-            return tiles
 
         w_kv = jnp.concatenate([w_k, w_v], axis=1)
         kv_part = tp(jnp.concatenate([own_part(w_k, 0), own_part(w_v, 0)], axis=1), 1)
@@ -236,13 +232,13 @@
         a_far_near = tp(kv_b_far, 1)
         far_a = hops(kv_a_far, a_far_near)
         b_far_near = tp(kv_a_far, 1)
-        far_b = direct(kv_b_far, after(b_far_near, far_a[3]))
+        far_b = hops(kv_b_far, b_far_near)
         x_two = after(x_two, kv_a_far, kv_b_far)
         q_a = far(2, w_q, [q_a_own])
         q_b = far(3, w_q_par, [q_b_own])
         tiles_a += far_a
         tiles_b += far_b
-        o_far = after(tp(after(o_part, a_far_near), 2), *far_a, b_far_near)
+        o_far = after(tp(after(o_part, a_far_near), 2), *far_a, *far_b)
         o_cross = tp(o_far, 1)
         w_far = lax.all_gather(o_far, ("dp", "cp"), axis=0)
 
@@ -252,11 +248,11 @@
         out_a = attend(q_a, [q_b, o_far], tiles_a)
         got_a = tp(out_a[:T], 2)
         w_cross = lax.all_gather(after(o_cross, out_a), ("dp", "cp"), axis=0)
-        tiles_b = tiles_b[:8] + [after(t, out_a) for t in tiles_b[8:]]
         out_b, got_b = [out_a], []
         for head in range(w_k.shape[1] // D):
             out_b.append(attend(q_b, out_b[-1:], tiles_b, heads=(head,)))
             got_b.append(tp(out_b[-1][:T], 2))
-        return out_proj([([out_a], 1), (out_b[1:], 1), ([got_a], 0), (got_b, 0)], [w_o, w_near, w_far, w_cross])
+        y_part = out_proj([([out_a], 1), (out_b[1:], 1), ([got_a], 0)], [w_o, w_near, w_far], jnp.float32)
+        return out_proj([(got_b, 0)], [w_cross], jnp.bfloat16, part=y_part)
 
     return jax.shard_map(local_layer, mesh=mesh, in_specs=(row_spec, P(None, "tp"), P(None, "tp"), P(None, "tp"), P("tp", None)), out_specs=row_spec, check_vma=False)

time: 667 us -> 608 us (0.912)
  waiting for transfers between devices: 396 us -> 331 us
  Pallas kernels: 124 us -> 133 us
    ppermute x38, waiting for transfers between devices: 396 us -> 331 us  [swap(): return lax.ppermute(x, axis, [(i, i ^ bit) for i in range(size)])]
    pallas_call x1 -> x2, Pallas kernels: 23.4 us -> 32.2 us  [out_proj(): pl.pallas_call(functools.partial(out_kernel, counts=[len(group) for group...]
    unnamed x81 -> x77, local copies, waits for them, and re-layouts: 13.6 us -> 11.6 us
  transfers between devices with their start and end apart: 43 -> 43, of which waited for: 19 -> 15; matrix products, arithmetic and copies ran while one was open for 12% -> 13% of each run, Pallas kernels for 15% -> 20%
where the time goes in v3:
time: 608 us; the launch traced here: 603 us
  waiting for transfers between devices  331 us (54%)
  Pallas kernels  133 us (22%)
  matrix products  63.1 us (10%)
  starting transfers between devices  34.2 us (6%)
  local copies, waits for them, and re-layouts  24.3 us (4%)
  between operations  13.9 us (2%)
    ppermute x38, waiting for transfers between devices, swap(): return lax.ppermute(x, axis, [(i, i ^ bit) for i in range(size)])  331 us
    pallas_call x3, Pallas kernels, flash(): pl.pallas_call(functools.partial(flash_kernel, group=group, cp_size=cp_si...  101 us
    dot_general x12, matrix products, project(): jnp.dot(x, w, preferred_element_type=jnp.float32).astype(jnp.bfloat16)  63.1 us
    ppermute x38, starting transfers between devices, swap(): return lax.ppermute(x, axis, [(i, i ^ bit) for i in range(size)])  33.7 us
    pallas_call x2, Pallas kernels, out_proj(): pl.pallas_call(functools.partial(out_kernel, counts=[len(group) for group...  32.2 us
  transfers between devices with their start and end apart: 43, of which 15 were waited for; matrix products, arithmetic and copies ran while one was open for 13% of the time, Pallas kernels for 20%

profile of v3, /device:TPU:0, one launch (start us, length us, event | category | flops | bytes accessed | tf_op | source)
XLA Modules:
  0.0 602.8 jit_solution(16003316071131113519)
XLA Ops:
  7.8 3.1 collective-permute-start.2
  10.9 1.8 constant_dynamic-update-slice_fusion.1
  12.9 3.1 fusion.2.refs_0_
  16.0 6.8 %collective-permute-done.2 = bf16[512,512]{1,0:T(8,128)(2,1)S(1)} collective-permute-done((bf16[512,512]{1,0:T(8,128)(2,1)S(1)}, bf16[512,512]{1,0:T(8,128)(2,1)S(1)}, u32[]{:S(2)}, u32[]{:S(2)}) %collective-permute-start.2) | collective-permute-done | bytes 524320 | tf_op jit(solution)/shard_map/ppermute | solution.py:166
  23.7 1.3 constant_dynamic-slice_fusion.3
  25.0 1.8 collective-permute-start
  26.8 22.6 %collective-permute-done = bf16[512,1024]{1,0:T(8,128)(2,1)S(1)} collective-permute-done((bf16[512,1024]{1,0:T(8,128)(2,1)S(1)}, bf16[512,1024]{1,0:T(8,128)(2,1)S(1)}, u32[]{:S(2)}, u32[]{:S(2)}) %collective-permute-start) | collective-permute-done | bytes 1048608 | tf_op jit(solution)/shard_map/ppermute | solution.py:166
  50.5 2.8 fusion.6
  53.3 2.5 collective-permute-start.1
  55.8 1.6 collective-permute-start.11
  57.4 1.3 constant_dynamic-slice_fusion
  59.2 85.9 %collective-permute-done.1 = bf16[256,4096]{1,0:T(8,128)(2,1)S(1)} collective-permute-done((bf16[256,4096]{1,0:T(8,128)(2,1)S(1)}, bf16[256,4096]{1,0:T(8,128)(2,1)S(1)}, u32[]{:S(2)}, u32[]{:S(2)}) %collective-permute-start.1) | collective-permute-done | bytes 2097184 | tf_op jit(solution)/shard_map/ppermute | solution.py:166
  147.6 5.8 fusion.3.refs_0_
  155.4 6.2 %collective-permute-done.5.refs_2_ = bf16[512,512]{1,0:T(8,128)(2,1)} collective-permute-done((bf16[512,512]{1,0:T(8,128)(2,1)}, bf16[512,512]{1,0:T(8,128)(2,1)}, u32[]{:S(2)}, u32[]{:S(2)}) %collective-permute-start.5) | collective-permute-done | bytes 524320 | tf_op jit(solution)/shard_map/ppermute | solution.py:166
  161.5 5.2 collective-permute-done.4.refs_1_
  167.6 1.3 collective-permute-start.12
  169.6 1.8 collective-permute-done.13.refs_3_
  172.0 10.5 %collective-permute-done.12.refs_2_ = bf16[512,512]{1,0:T(8,128)(2,1)S(1)} collective-permute-done((bf16[512,512]{1,0:T(8,128)(2,1)}, bf16[512,512]{1,0:T(8,128)(2,1)S(1)}, u32[]{:S(2)}, u32[]{:S(2)}) %collective-permute-start.12) | collective-permute-done | bytes 524320 | tf_op jit(solution)/shard_map/ppermute | solution.py:166
  183.4 10.2 %collective-permute-done.6.refs_3_ = bf16[512,512]{1,0:T(8,128)(2,1)S(1)} collective-permute-done((bf16[512,512]{1,0:T(8,128)(2,1)}, bf16[512,512]{1,0:T(8,128)(2,1)S(1)}, u32[]{:S(2)}, u32[]{:S(2)}) %collective-permute-start.6) | collective-permute-done | bytes 524320 | tf_op jit(solution)/shard_map/ppermute | solution.py:166
  196.2 10.2 %convolution_convert_fusion.1 = bf16[512,1024]{1,0:T(8,128)(2,1)} fusion(bf16[512,4096]{1,0:T(8,128)(2,1)} %param.5, bf16[4096,1024]{1,0:T(8,128)(2,1)} %param.6), kind=kOutput, calls=%fused_computation.3 | convolution fusion | flops 4295491584 | bytes 13631488 | tf_op jit(solution)/shard_map/dot_general | solution.py:170
  206.5 6.7 %convolution_convert_fusion.7 = bf16[256,1024]{1,0:T(8,128)(2,1)} fusion(bf16[256,4096]{1,0:T(8,128)(2,1)S(1)} %copy-done.20, bf16[4096,1024]{1,0:T(8,128)(2,1)} %param.6), kind=kOutput, calls=%fused_computation.10 | convolution fusion | flops 2147745792 | bytes 11010048 | tf_op jit(solution)/shard_map/dot_general | solution.py:170
  213.2 3.1 collective-permute-start.3
  217.5 3.1 fusion.1
  220.7 5.5 fusion
  226.2 81.2 %collective-permute-done.3 = bf16[256,4096]{1,0:T(8,128)(2,1)S(1)} collective-permute-done((bf16[256,4096]{1,0:T(8,128)(2,1)S(1)}, bf16[256,4096]{1,0:T(8,128)(2,1)S(1)}, u32[]{:S(2)}, u32[]{:S(2)}) %collective-permute-start.3) | collective-permute-done | bytes 2097184 | tf_op jit(solution)/shard_map/ppermute | solution.py:166
  309.5 12.5 %convolution_convert_fusion.11 = bf16[256,512]{1,0:T(8,128)(2,1)S(1)} fusion(bf16[256,4096]{1,0:T(8,128)(2,1)S(1)} %collective-permute-done.3, bf16[4096,512]{1,0:T(8,128)(2,1)S(1)} %copy-done.5), kind=kOutput, calls=%fused_computation.17 | convolution fusion | flops 1073872896 | bytes 6553600 | tf_op jit(solution)/shard_map/dot_general | solution.py:170
  322.8 1.4 collective-permute-start.26
  325.5 11.4 %collective-permute-done.20.refs_10_ = bf16[512,512]{1,0:T(8,128)(2,1)S(1)} collective-permute-done((bf16[512,512]{1,0:T(8,128)(2,1)S(1)}, bf16[512,512]{1,0:T(8,128)(2,1)S(1)}, u32[]{:S(2)}, u32[]{:S(2)}) %collective-permute-start.20) | collective-permute-done | bytes 524320 | tf_op jit(solution)/shard_map/ppermute | solution.py:166
  336.9 3.4 collective-permute-start.19
  341.0 7.2 %collective-permute-done.27.refs_10_ = bf16[512,512]{1,0:T(8,128)(2,1)S(1)} collective-permute-done((bf16[512,512]{1,0:T(8,128)(2,1)S(1)}, bf16[512,512]{1,0:T(8,128)(2,1)S(1)}, u32[]{:S(2)}, u32[]{:S(2)}) %collective-permute-start.27) | collective-permute-done | bytes 524320 | tf_op jit(solution)/shard_map/ppermute | solution.py:166
  348.9 10.6 %collective-permute-done.21.refs_11_ = bf16[512,512]{1,0:T(8,128)(2,1)} collective-permute-done((bf16[512,512]{1,0:T(8,128)(2,1)S(1)}, bf16[512,512]{1,0:T(8,128)(2,1)}, u32[]{:S(2)}, u32[]{:S(2)}) %collective-permute-start.21) | collective-permute-done | bytes 524320 | tf_op jit(solution)/shard_map/ppermute | solution.py:166
  360.1 9.4 %collective-permute-done.28.refs_11_ = bf16[512,512]{1,0:T(8,128)(2,1)} collective-permute-done((bf16[512,512]{1,0:T(8,128)(2,1)S(1)}, bf16[512,512]{1,0:T(8,128)(2,1)}, u32[]{:S(2)}, u32[]{:S(2)}) %collective-permute-start.28) | collective-permute-done | bytes 524320 | tf_op jit(solution)/shard_map/ppermute | solution.py:166
  371.1 12.8 %collective-permute-done.19 = bf16[1024,512]{1,0:T(8,128)(2,1)} collective-permute-done((bf16[1024,512]{1,0:T(8,128)(2,1)S(1)}, bf16[1024,512]{1,0:T(8,128)(2,1)}, u32[]{:S(2)}, u32[]{:S(2)}) %collective-permute-start.19) | collective-permute-done | bytes 1048608 | tf_op jit(solution)/shard_map/ppermute | solution.py:166
  384.0 6.4 %convolution_convert_fusion.6 = bf16[256,1024]{1,0:T(8,128)(2,1)S(1)} fusion(bf16[256,4096]{1,0:T(8,128)(2,1)} %copy-done.17, bf16[4096,1024]{1,0:T(8,128)(2,1)} %all-gather.9.cloned.1.call-done), kind=kOutput, calls=%fused_computation.9 | convolution fusion | flops 2147745792 | bytes 11010048 | tf_op jit(solution)/shard_map/dot_general | solution.py:170
  390.5 1.5 pad_maximum_fusion.q_ref
  393.0 5.9 convolution_convert_fusion.5
  398.9 1.5 pad_maximum_fusion.1.q_ref
  400.6 47.9 %shard_map.55.refs_0_ = bf16[1024,1024]{1,0:T(8,128)(2,1)} custom-call(bf16[1024,1024]{1,0:T(8,128)(2,1)} %pad_maximum_fusion.1.q_ref, bf16[512,512]{1,0:T(8,128)(2,1)} %fusion.2.refs_0_, bf16[512,512]{1,0:T(8,128)(2,1)} %copy-done.23, bf16[512,512]{1,0:T(8,128)(2,1)} %collective-permute-done.5.refs_2_, bf16[512,512]{1,0:T(8,128)(2,1)} %copy-done.27, ...), custom_call_target="tpu_custom_call" | custom-call | flops 20000000000 | bytes 12582912 | tf_op jit(solution)/shard_map/pallas_call | solution.py:111
  448.5 26.5 %shard_map.56.refs_1_ = bf16[1024,512]{1,0:T(8,128)(2,1)} custom-call(bf16[1024,1024]{1,0:T(8,128)(2,1)} %pad_maximum_fusion.q_ref, bf16[512,512]{1,0:T(8,128)(2,1)} %copy-done.21, bf16[512,512]{1,0:T(8,128)(2,1)} %collective-permute-done.11.refs_1_, bf16[512,512]{1,0:T(8,128)(2,1)} %copy-done.22, bf16[512,512]{1,0:T(8,128)(2,1)} %collective-permute-done.13.refs_3_, ...), custom_call_target="tpu_custom_call" | custom-call | flops 20000000000 | bytes 12582912 | tf_op jit(solution)/shard_map/pallas_call | solution.py:111
  475.0 1.9 slice.20
  476.9 2.3 slice.22
  479.2 3.4 collective-permute-start.33
  482.6 26.5 %shard_map.57.refs_2_ = bf16[1024,512]{1,0:T(8,128)(2,1)} custom-call(bf16[1024,1024]{1,0:T(8,128)(2,1)} %pad_maximum_fusion.q_ref, bf16[512,512]{1,0:T(8,128)(2,1)} %copy-done.21, bf16[512,512]{1,0:T(8,128)(2,1)} %collective-permute-done.11.refs_1_, bf16[512,512]{1,0:T(8,128)(2,1)} %copy-done.22, bf16[512,512]{1,0:T(8,128)(2,1)} %collective-permute-done.13.refs_3_, ...), custom_call_target="tpu_custom_call" | custom-call | flops 20000000000 | bytes 12582912 | tf_op jit(solution)/shard_map/pallas_call | solution.py:111
  509.1 1.9 slice.21
  511.0 2.9 collective-permute-start.34
  513.8 49.2 %collective-permute-done.36.refs_3_ = bf16[512,1024]{1,0:T(8,128)(2,1)} collective-permute-done((bf16[512,1024]{1,0:T(8,128)(2,1)}, bf16[512,1024]{1,0:T(8,128)(2,1)}, u32[]{:S(2)}, u32[]{:S(2)}) %collective-permute-start.36) | collective-permute-done | bytes 1048608 | tf_op jit(solution)/shard_map/ppermute | solution.py:166
  563.1 20.2 %shard_map.58.refs_3_ = f32[512,4096]{1,0:T(8,128)} custom-call(bf16[1024,1024]{1,0:T(8,128)(2,1)} %shard_map.55.refs_0_, bf16[1024,512]{1,0:T(8,128)(2,1)} %shard_map.56.refs_1_, bf16[1024,512]{1,0:T(8,128)(2,1)} %shard_map.57.refs_2_, bf16[512,1024]{1,0:T(8,128)(2,1)} %collective-permute-done.36.refs_3_, bf16[1024,4096]{1,0:T(8,128)(2,1)} %refs_4_.1, ...), custom_call_target="tpu_custom_call" | custom-call | flops 12884901888 | bytes 25165824 | tf_op jit(solution)/shard_map/pallas_call | solution.py:152
  584.1 12.0 %shard_map.59 = bf16[512,4096]{1,0:T(8,128)(2,1)} custom-call(bf16[512,512]{1,0:T(8,128)(2,1)} %copy-done.9, bf16[512,512]{1,0:T(8,128)(2,1)} %collective-permute-done.34.refs_1_, bf16[8,1024,512]{2,1,0:T(8,128)(2,1)} %bitcast.39, f32[512,4096]{1,0:T(8,128)} %shard_map.58.refs_3_), custom_call_target="tpu_custom_call" | custom-call | flops 4294967296 | bytes 8388608 | tf_op jit(solution)/shard_map/pallas_call | solution.py:152
  (150 shorter events, 24.9 us)
Async XLA Ops:
  6.5 141.0 %all-gather.11.cloned.1.call-start = ((), (), s32[]{:S(2)}) async-start(), calls=%async_computation.1 | async-start | bytes 4718592 | tf_op jit(solution)/shard_map/all_gather | solution.py:209
  7.8 15.0 %collective-permute-start.2 = (bf16[512,512]{1,0:T(8,128)(2,1)S(1)}, bf16[512,512]{1,0:T(8,128)(2,1)S(1)}, u32[]{:S(2)}, u32[]{:S(2)}) collective-permute-start(bf16[512,512]{1,0:T(8,128)(2,1)S(1)} %pad_maximum_fusion.2), channel_id=1, source_target_pairs={{0,4},{4,0},{8,12},{12,8},{1,5},{5,1},{9,13},{13,9},{2,6},{6,2},{1... | collective-permute-start | bytes 1572872 | tf_op jit(solution)/shard_map/ppermute | solution.py:166
  23.7 172.1 %all-gather.9.cloned.1.call-start = ((), (), s32[]{:S(2)}) async-start(), calls=%async_computation | async-start | bytes 9437184 | tf_op jit(solution)/shard_map/all_gather | solution.py:210
  25.0 24.4 %collective-permute-start = (bf16[512,1024]{1,0:T(8,128)(2,1)S(1)}, bf16[512,1024]{1,0:T(8,128)(2,1)S(1)}, u32[]{:S(2)}, u32[]{:S(2)}) collective-permute-start(bf16[512,1024]{1,0:T(8,128)(2,1)S(1)} %constant_dynamic-slice_fusion.3), channel_id=1, source_target_pairs={{0,4},{4,0},{8,12},{12,8},{1,5},{5,1},{9,13},{13,9},{2,6},{6,2},{1... | collective-permute-start | bytes 3145736 | tf_op jit(solution)/shard_map/ppermute | solution.py:166
  50.4 512.6 %all-gather.15.cloned.1.call-start = ((), (), s32[]{:S(2)}) async-start(), calls=%async_computation.3 | async-start | bytes 9437184 | tf_op jit(solution)/shard_map/all_gather | solution.py:224
  50.5 94.6 %copy-start.4 = (bf16[4096,512]{1,0:T(8,128)(2,1)S(1)}, bf16[4096,512]{1,0:T(8,128)(2,1)}, u32[]{:S(2)}) copy-start(bf16[4096,512]{1,0:T(8,128)(2,1)} %copy-done.3) | copy-start | bytes 12582916
  53.3 91.8 %collective-permute-start.1 = (bf16[256,4096]{1,0:T(8,128)(2,1)S(1)}, bf16[256,4096]{1,0:T(8,128)(2,1)S(1)}, u32[]{:S(2)}, u32[]{:S(2)}) collective-permute-start(bf16[256,4096]{1,0:T(8,128)(2,1)S(1)} %get-tuple-element.37), channel_id=1, source_target_pairs={{0,8},{4,12},{8,0},{12,4},{1,9},{5,13},{9,1},{13,5},{2,10},{6,14},... | collective-permute-start | bytes 6291464 | tf_op jit(solution)/shard_map/ppermute | solution.py:166
  55.8 99.1 %collective-permute-start.11 = (bf16[512,512]{1,0:T(8,128)(2,1)}, bf16[512,512]{1,0:T(8,128)(2,1)}, u32[]{:S(2)}, u32[]{:S(2)}) collective-permute-start(bf16[512,512]{1,0:T(8,128)(2,1)} %fusion.2.refs_0_), channel_id=1, source_target_pairs={{0,4},{4,0},{8,12},{12,8},{1,5},{5,1},{9,13},{13,9},{2,6},{6,2},{1... | collective-permute-start | bytes 1572872 | tf_op jit(solution)/shard_map/ppermute | solution.py:166
  58.7 108.9 %collective-permute-start.37 = (bf16[1024,512]{1,0:T(8,128)(2,1)S(1)}, bf16[1024,512]{1,0:T(8,128)(2,1)}, u32[]{:S(2)}, u32[]{:S(2)}) collective-permute-start(bf16[1024,512]{1,0:T(8,128)(2,1)S(1)} %constant_dynamic-slice_fusion), channel_id=1, source_target_pairs={{0,4},{4,0},{8,12},{12,8},{1,5},{5,1},{9,13},{13,9},{2,6},{6,2},{1... | collective-permute-start | bytes 3145736 | tf_op jit(solution)/shard_map/ppermute | solution.py:166
  146.4 15.1 %collective-permute-start.5 = (bf16[512,512]{1,0:T(8,128)(2,1)}, bf16[512,512]{1,0:T(8,128)(2,1)}, u32[]{:S(2)}, u32[]{:S(2)}) collective-permute-start(bf16[512,512]{1,0:T(8,128)(2,1)} %fusion.2.refs_0_), channel_id=1, source_target_pairs={{0,2},{1,3},{2,0},{3,1},{4,6},{5,7},{6,4},{7,5},{8,10},{9,11},{10,... | collective-permute-start | bytes 1572872 | tf_op jit(solution)/shard_map/ppermute | solution.py:166
  154.2 12.5 %collective-permute-start.4 = (bf16[512,512]{1,0:T(8,128)(2,1)S(1)}, bf16[512,512]{1,0:T(8,128)(2,1)S(1)}, u32[]{:S(2)}, u32[]{:S(2)}) collective-permute-start(bf16[512,512]{1,0:T(8,128)(2,1)S(1)} %fusion.3.refs_0_), channel_id=1, source_target_pairs={{0,4},{4,0},{8,12},{12,8},{1,5},{5,1},{9,13},{13,9},{2,6},{6,2},{1... | collective-permute-start | bytes 1572872 | tf_op jit(solution)/shard_map/ppermute | solution.py:166
  154.9 14.0 %collective-permute-start.7 = (bf16[512,512]{1,0:T(8,128)(2,1)}, bf16[512,512]{1,0:T(8,128)(2,1)}, u32[]{:S(2)}, u32[]{:S(2)}) collective-permute-start(bf16[512,512]{1,0:T(8,128)(2,1)} %fusion.2.refs_0_), channel_id=1, source_target_pairs={{0,1},{1,0},{2,3},{3,2},{4,5},{5,4},{6,7},{7,6},{8,9},{9,8},{10,11... | collective-permute-start | bytes 1572872 | tf_op jit(solution)/shard_map/ppermute | solution.py:166
  154.9 16.6 %collective-permute-start.13 = (bf16[512,512]{1,0:T(8,128)(2,1)}, bf16[512,512]{1,0:T(8,128)(2,1)}, u32[]{:S(2)}, u32[]{:S(2)}) collective-permute-start(bf16[512,512]{1,0:T(8,128)(2,1)} %collective-permute-done.11.refs_1_), channel_id=1, source_target_pairs={{0,2},{1,3},{2,0},{3,1},{4,6},{5,7},{6,4},{7,5},{8,10},{9,11},{10,... | collective-permute-start | bytes 1572872 | tf_op jit(solution)/shard_map/ppermute | solution.py:166
  161.5 9.9 %collective-permute-start.15 = (bf16[512,512]{1,0:T(8,128)(2,1)}, bf16[512,512]{1,0:T(8,128)(2,1)}, u32[]{:S(2)}, u32[]{:S(2)}) collective-permute-start(bf16[512,512]{1,0:T(8,128)(2,1)} %collective-permute-done.11.refs_1_), channel_id=1, source_target_pairs={{0,1},{1,0},{2,3},{3,2},{4,5},{5,4},{6,7},{7,6},{8,9},{9,8},{10,11... | collective-permute-start | bytes 1572872 | tf_op jit(solution)/shard_map/ppermute | solution.py:166
  167.6 4.4 collective-permute-start.9
  167.6 15.0 %collective-permute-start.12 = (bf16[512,512]{1,0:T(8,128)(2,1)}, bf16[512,512]{1,0:T(8,128)(2,1)S(1)}, u32[]{:S(2)}, u32[]{:S(2)}) collective-permute-start(bf16[512,512]{1,0:T(8,128)(2,1)} %copy-done.21), channel_id=1, source_target_pairs={{0,2},{1,3},{2,0},{3,1},{4,6},{5,7},{6,4},{7,5},{8,10},{9,11},{10,... | collective-permute-start | bytes 1572872 | tf_op jit(solution)/shard_map/ppermute | solution.py:166
  168.8 24.7 %collective-permute-start.6 = (bf16[512,512]{1,0:T(8,128)(2,1)}, bf16[512,512]{1,0:T(8,128)(2,1)S(1)}, u32[]{:S(2)}, u32[]{:S(2)}) collective-permute-start(bf16[512,512]{1,0:T(8,128)(2,1)} %copy-done.23), channel_id=1, source_target_pairs={{0,2},{1,3},{2,0},{3,1},{4,6},{5,7},{6,4},{7,5},{8,10},{9,11},{10,... | collective-permute-start | bytes 1572872 | tf_op jit(solution)/shard_map/ppermute | solution.py:166
  171.4 22.1 %collective-permute-start.17 = (bf16[512,512]{1,0:T(8,128)(2,1)}, bf16[512,512]{1,0:T(8,128)(2,1)S(1)}, u32[]{:S(2)}, u32[]{:S(2)}) collective-permute-start(bf16[512,512]{1,0:T(8,128)(2,1)} %collective-permute-done.13.refs_3_), channel_id=1, source_target_pairs={{0,1},{1,0},{2,3},{3,2},{4,5},{5,4},{6,7},{7,6},{8,9},{9,8},{10,11... | collective-permute-start | bytes 1572872 | tf_op jit(solution)/shard_map/ppermute | solution.py:166
  171.4 22.2 %collective-permute-start.14 = (bf16[512,512]{1,0:T(8,128)(2,1)}, bf16[512,512]{1,0:T(8,128)(2,1)S(1)}, u32[]{:S(2)}, u32[]{:S(2)}) collective-permute-start(bf16[512,512]{1,0:T(8,128)(2,1)} %copy-done.21), channel_id=1, source_target_pairs={{0,1},{1,0},{2,3},{3,2},{4,5},{5,4},{6,7},{7,6},{8,9},{9,8},{10,11... | collective-permute-start | bytes 1572872 | tf_op jit(solution)/shard_map/ppermute | solution.py:166
  172.0 21.7 %collective-permute-start.8 = (bf16[512,512]{1,0:T(8,128)(2,1)}, bf16[512,512]{1,0:T(8,128)(2,1)S(1)}, u32[]{:S(2)}, u32[]{:S(2)}) collective-permute-start(bf16[512,512]{1,0:T(8,128)(2,1)} %copy-done.23), channel_id=1, source_target_pairs={{0,1},{1,0},{2,3},{3,2},{4,5},{5,4},{6,7},{7,6},{8,9},{9,8},{10,11... | collective-permute-start | bytes 1572872 | tf_op jit(solution)/shard_map/ppermute | solution.py:166
  183.4 10.3 %collective-permute-start.16 = (bf16[512,512]{1,0:T(8,128)(2,1)S(1)}, bf16[512,512]{1,0:T(8,128)(2,1)S(1)}, u32[]{:S(2)}, u32[]{:S(2)}) collective-permute-start(bf16[512,512]{1,0:T(8,128)(2,1)S(1)} %collective-permute-done.12.refs_2_), channel_id=1, source_target_pairs={{0,1},{1,0},{2,3},{3,2},{4,5},{5,4},{6,7},{7,6},{8,9},{9,8},{10,11... | collective-permute-start | bytes 1572872 | tf_op jit(solution)/shard_map/ppermute | solution.py:166
  193.6 2.2 collective-permute-start.10
  195.8 367.3 %all-gather.17.cloned.1.call-start = ((), (), s32[]{:S(2)}) async-start(), calls=%async_computation.4 | async-start | bytes 9437184 | tf_op jit(solution)/shard_map/all_gather | solution.py:243
  213.2 94.2 %collective-permute-start.3 = (bf16[256,4096]{1,0:T(8,128)(2,1)S(1)}, bf16[256,4096]{1,0:T(8,128)(2,1)S(1)}, u32[]{:S(2)}, u32[]{:S(2)}) collective-permute-start(bf16[256,4096]{1,0:T(8,128)(2,1)S(1)} %get-tuple-element.23), channel_id=1, source_target_pairs={{0,8},{4,12},{8,0},{12,4},{1,9},{5,13},{9,1},{13,5},{2,10},{6,14},... | collective-permute-start | bytes 6291464 | tf_op jit(solution)/shard_map/ppermute | solution.py:166
  226.2 83.3 %copy-start.5 = (bf16[4096,512]{1,0:T(8,128)(2,1)S(1)}, bf16[4096,512]{1,0:T(8,128)(2,1)}, u32[]{:S(2)}) copy-start(bf16[4096,512]{1,0:T(8,128)(2,1)} %copy-done.3) | copy-start | bytes 12582916
  308.6 16.8 %collective-permute-start.18 = (bf16[512,512]{1,0:T(8,128)(2,1)S(1)}, bf16[512,512]{1,0:T(8,128)(2,1)S(1)}, u32[]{:S(2)}, u32[]{:S(2)}) collective-permute-start(bf16[512,512]{1,0:T(8,128)(2,1)S(1)} %pad_maximum_fusion.4.refs_8_), channel_id=1, source_target_pairs={{0,4},{4,0},{8,12},{12,8},{1,5},{5,1},{9,13},{13,9},{2,6},{6,2},{1... | collective-permute-start | bytes 1572872 | tf_op jit(solution)/shard_map/ppermute | solution.py:166
  322.1 68.4 %copy-start.11 = (bf16[512,512]{1,0:T(8,128)(2,1)}, bf16[512,512]{1,0:T(8,128)(2,1)S(1)}, u32[]{:S(2)}) copy-start(bf16[512,512]{1,0:T(8,128)(2,1)S(1)} %pad_maximum_fusion.3.refs_8_) | copy-start | bytes 1572868
  322.1 14.9 %collective-permute-start.20 = (bf16[512,512]{1,0:T(8,128)(2,1)S(1)}, bf16[512,512]{1,0:T(8,128)(2,1)S(1)}, u32[]{:S(2)}, u32[]{:S(2)}) collective-permute-start(bf16[512,512]{1,0:T(8,128)(2,1)S(1)} %pad_maximum_fusion.3.refs_8_), channel_id=1, source_target_pairs={{0,2},{1,3},{2,0},{3,1},{4,6},{5,7},{6,4},{7,5},{8,10},{9,11},{10,... | collective-permute-start | bytes 1572872 | tf_op jit(solution)/shard_map/ppermute | solution.py:166
  322.8 17.5 %collective-permute-start.22 = (bf16[512,512]{1,0:T(8,128)(2,1)S(1)}, bf16[512,512]{1,0:T(8,128)(2,1)S(1)}, u32[]{:S(2)}, u32[]{:S(2)}) collective-permute-start(bf16[512,512]{1,0:T(8,128)(2,1)S(1)} %pad_maximum_fusion.3.refs_8_), channel_id=1, source_target_pairs={{0,1},{1,0},{2,3},{3,2},{4,5},{5,4},{6,7},{7,6},{8,9},{9,8},{10,11... | collective-permute-start | bytes 1572872 | tf_op jit(solution)/shard_map/ppermute | solution.py:166
  322.8 18.2 %collective-permute-start.26 = (bf16[512,512]{1,0:T(8,128)(2,1)S(1)}, bf16[512,512]{1,0:T(8,128)(2,1)S(1)}, u32[]{:S(2)}, u32[]{:S(2)}) collective-permute-start(bf16[512,512]{1,0:T(8,128)(2,1)S(1)} %pad_maximum_fusion.3.refs_8_), channel_id=1, source_target_pairs={{0,4},{4,0},{8,12},{12,8},{1,5},{5,1},{9,13},{13,9},{2,6},{6,2},{1... | collective-permute-start | bytes 1572872 | tf_op jit(solution)/shard_map/ppermute | solution.py:166
  324.2 23.9 %collective-permute-start.27 = (bf16[512,512]{1,0:T(8,128)(2,1)S(1)}, bf16[512,512]{1,0:T(8,128)(2,1)S(1)}, u32[]{:S(2)}, u32[]{:S(2)}) collective-permute-start(bf16[512,512]{1,0:T(8,128)(2,1)S(1)} %pad_maximum_fusion.4.refs_8_), channel_id=1, source_target_pairs={{0,2},{1,3},{2,0},{3,1},{4,6},{5,7},{6,4},{7,5},{8,10},{9,11},{10,... | collective-permute-start | bytes 1572872 | tf_op jit(solution)/shard_map/ppermute | solution.py:166
  325.4 44.1 %copy-start.32 = (bf16[512,512]{1,0:T(8,128)(2,1)}, bf16[512,512]{1,0:T(8,128)(2,1)S(1)}, u32[]{:S(2)}) copy-start(bf16[512,512]{1,0:T(8,128)(2,1)S(1)} %collective-permute-done.18.refs_9_) | copy-start | bytes 1572868
  325.4 22.7 %collective-permute-start.29 = (bf16[512,512]{1,0:T(8,128)(2,1)S(1)}, bf16[512,512]{1,0:T(8,128)(2,1)S(1)}, u32[]{:S(2)}, u32[]{:S(2)}) collective-permute-start(bf16[512,512]{1,0:T(8,128)(2,1)S(1)} %pad_maximum_fusion.4.refs_8_), channel_id=1, source_target_pairs={{0,1},{1,0},{2,3},{3,2},{4,5},{5,4},{6,7},{7,6},{8,9},{9,8},{10,11... | collective-permute-start | bytes 1572872 | tf_op jit(solution)/shard_map/ppermute | solution.py:166
  336.9 47.0 %collective-permute-start.19 = (bf16[1024,512]{1,0:T(8,128)(2,1)S(1)}, bf16[1024,512]{1,0:T(8,128)(2,1)}, u32[]{:S(2)}, u32[]{:S(2)}) collective-permute-start(bf16[1024,512]{1,0:T(8,128)(2,1)S(1)} %constant_dynamic-slice_fusion), channel_id=1, source_target_pairs={{0,8},{4,12},{8,0},{12,4},{1,9},{5,13},{9,1},{13,5},{2,10},{6,14},... | collective-permute-start | bytes 3145736 | tf_op jit(solution)/shard_map/ppermute | solution.py:166
  340.3 19.2 %collective-permute-start.21 = (bf16[512,512]{1,0:T(8,128)(2,1)S(1)}, bf16[512,512]{1,0:T(8,128)(2,1)}, u32[]{:S(2)}, u32[]{:S(2)}) collective-permute-start(bf16[512,512]{1,0:T(8,128)(2,1)S(1)} %collective-permute-done.18.refs_9_), channel_id=1, source_target_pairs={{0,2},{1,3},{2,0},{3,1},{4,6},{5,7},{6,4},{7,5},{8,10},{9,11},{10,... | collective-permute-start | bytes 1572872 | tf_op jit(solution)/shard_map/ppermute | solution.py:166
  341.0 49.5 %copy-start.29 = (bf16[512,512]{1,0:T(8,128)(2,1)}, bf16[512,512]{1,0:T(8,128)(2,1)S(1)}, u32[]{:S(2)}) copy-start(bf16[512,512]{1,0:T(8,128)(2,1)S(1)} %collective-permute-done.26.refs_9_) | copy-start | bytes 1572868
  341.0 18.5 %collective-permute-start.23 = (bf16[512,512]{1,0:T(8,128)(2,1)S(1)}, bf16[512,512]{1,0:T(8,128)(2,1)}, u32[]{:S(2)}, u32[]{:S(2)}) collective-permute-start(bf16[512,512]{1,0:T(8,128)(2,1)S(1)} %collective-permute-done.18.refs_9_), channel_id=1, source_target_pairs={{0,1},{1,0},{2,3},{3,2},{4,5},{5,4},{6,7},{7,6},{8,9},{9,8},{10,11... | collective-permute-start | bytes 1572872 | tf_op jit(solution)/shard_map/ppermute | solution.py:166
  348.2 11.9 %collective-permute-start.24 = (bf16[512,512]{1,0:T(8,128)(2,1)S(1)}, bf16[512,512]{1,0:T(8,128)(2,1)S(1)}, u32[]{:S(2)}, u32[]{:S(2)}) collective-permute-start(bf16[512,512]{1,0:T(8,128)(2,1)S(1)} %collective-permute-done.20.refs_10_), channel_id=1, source_target_pairs={{0,1},{1,0},{2,3},{3,2},{4,5},{5,4},{6,7},{7,6},{8,9},{9,8},{10,11... | collective-permute-start | bytes 1572872 | tf_op jit(solution)/shard_map/ppermute | solution.py:166
  348.2 21.3 %collective-permute-start.28 = (bf16[512,512]{1,0:T(8,128)(2,1)S(1)}, bf16[512,512]{1,0:T(8,128)(2,1)}, u32[]{:S(2)}, u32[]{:S(2)}) collective-permute-start(bf16[512,512]{1,0:T(8,128)(2,1)S(1)} %collective-permute-done.26.refs_9_), channel_id=1, source_target_pairs={{0,2},{1,3},{2,0},{3,1},{4,6},{5,7},{6,4},{7,5},{8,10},{9,11},{10,... | collective-permute-start | bytes 1572872 | tf_op jit(solution)/shard_map/ppermute | solution.py:166
  359.5 10.0 %collective-permute-start.30 = (bf16[512,512]{1,0:T(8,128)(2,1)S(1)}, bf16[512,512]{1,0:T(8,128)(2,1)S(1)}, u32[]{:S(2)}, u32[]{:S(2)}) collective-permute-start(bf16[512,512]{1,0:T(8,128)(2,1)S(1)} %collective-permute-done.26.refs_9_), channel_id=1, source_target_pairs={{0,1},{1,0},{2,3},{3,2},{4,5},{5,4},{6,7},{7,6},{8,9},{9,8},{10,11... | collective-permute-start | bytes 1572872 | tf_op jit(solution)/shard_map/ppermute | solution.py:166
  359.5 10.0 %collective-permute-start.31 = (bf16[512,512]{1,0:T(8,128)(2,1)S(1)}, bf16[512,512]{1,0:T(8,128)(2,1)S(1)}, u32[]{:S(2)}, u32[]{:S(2)}) collective-permute-start(bf16[512,512]{1,0:T(8,128)(2,1)S(1)} %collective-permute-done.27.refs_10_), channel_id=1, source_target_pairs={{0,1},{1,0},{2,3},{3,2},{4,5},{5,4},{6,7},{7,6},{8,9},{9,8},{10,11... | collective-permute-start | bytes 1572872 | tf_op jit(solution)/shard_map/ppermute | solution.py:166
  360.0 23.9 %collective-permute-start.25 = (bf16[512,512]{1,0:T(8,128)(2,1)}, bf16[512,512]{1,0:T(8,128)(2,1)}, u32[]{:S(2)}, u32[]{:S(2)}) collective-permute-start(bf16[512,512]{1,0:T(8,128)(2,1)} %collective-permute-done.21.refs_11_), channel_id=1, source_target_pairs={{0,1},{1,0},{2,3},{3,2},{4,5},{5,4},{6,7},{7,6},{8,9},{9,8},{10,11... | collective-permute-start | bytes 1572872 | tf_op jit(solution)/shard_map/ppermute | solution.py:166
  369.5 14.4 %collective-permute-start.32 = (bf16[512,512]{1,0:T(8,128)(2,1)}, bf16[512,512]{1,0:T(8,128)(2,1)}, u32[]{:S(2)}, u32[]{:S(2)}) collective-permute-start(bf16[512,512]{1,0:T(8,128)(2,1)} %collective-permute-done.28.refs_11_), channel_id=1, source_target_pairs={{0,1},{1,0},{2,3},{3,2},{4,5},{5,4},{6,7},{7,6},{8,9},{9,8},{10,11... | collective-permute-start | bytes 1572872 | tf_op jit(solution)/shard_map/ppermute | solution.py:166
  384.0 199.3 %all-gather.13.cloned.1.call-start = ((), (), s32[]{:S(2)}) async-start(), calls=%async_computation.2 | async-start | bytes 9437184 | tf_op jit(solution)/shard_map/all_gather | solution.py:250
  400.4 48.1 %collective-permute-start.35 = (bf16[1024,512]{1,0:T(8,128)(2,1)}, bf16[1024,512]{1,0:T(8,128)(2,1)}, u32[]{:S(2)}, u32[]{:S(2)}) collective-permute-start(bf16[1024,512]{1,0:T(8,128)(2,1)} %collective-permute-done.19), channel_id=1, source_target_pairs={{0,4},{4,0},{8,12},{12,8},{1,5},{5,1},{9,13},{13,9},{2,6},{6,2},{1... | collective-permute-start | bytes 3145736 | tf_op jit(solution)/shard_map/ppermute | solution.py:166
  479.2 104.1 %collective-permute-start.33 = (bf16[512,512]{1,0:T(8,128)(2,1)}, bf16[512,512]{1,0:T(8,128)(2,1)S(1)}, u32[]{:S(2)}, u32[]{:S(2)}) collective-permute-start(bf16[512,512]{1,0:T(8,128)(2,1)} %slice.20), channel_id=1, source_target_pairs={{0,8},{4,12},{8,0},{12,4},{1,9},{5,13},{9,1},{13,5},{2,10},{6,14},... | collective-permute-start | bytes 1572872 | tf_op jit(solution)/shard_map/ppermute | solution.py:166
  482.6 80.5 %collective-permute-start.36 = (bf16[512,1024]{1,0:T(8,128)(2,1)}, bf16[512,1024]{1,0:T(8,128)(2,1)}, u32[]{:S(2)}, u32[]{:S(2)}) collective-permute-start(bf16[512,1024]{1,0:T(8,128)(2,1)} %slice.22), channel_id=1, source_target_pairs={{0,8},{4,12},{8,0},{12,4},{1,9},{5,13},{9,1},{13,5},{2,10},{6,14},... | collective-permute-start | bytes 3145736 | tf_op jit(solution)/shard_map/ppermute | solution.py:166
  511.0 72.3 %collective-permute-start.34 = (bf16[512,512]{1,0:T(8,128)(2,1)}, bf16[512,512]{1,0:T(8,128)(2,1)}, u32[]{:S(2)}, u32[]{:S(2)}) collective-permute-start(bf16[512,512]{1,0:T(8,128)(2,1)} %slice.21), channel_id=1, source_target_pairs={{0,8},{4,12},{8,0},{12,4},{1,9},{5,13},{9,1},{13,5},{2,10},{6,14},... | collective-permute-start | bytes 1572872 | tf_op jit(solution)/shard_map/ppermute | solution.py:166
  (33 other events, 236.6 us)
Sparse Core Ops, SparseCore 0:
  23.8 37.9 all-gather.10
  63.7 54.2 all-gather.8
  195.9 55.6 all-gather.14
  384.1 53.7 all-gather.16
  448.6 59.8 all-gather.12
